TPU v7x, 32 devices: a whole 2x2x4 slice. The times are simulated.
32 devices in a mesh: members: 2 (over x), zonal: 8 (over z, y), merid: 2 (over core).
Axes of the slice: x: 2, y: 2, z: 4, core: 2. Of those that a mesh axis runs over, the one named last changes fastest.
Arguments:
- height: float32 [256, 1024], P(('members', 'zonal'), 'merid'), parts along dimension 0, may hold values from -6 to 6
- transport_u: float32 [256, 1024], P(('members', 'zonal'), 'merid'), parts along dimension 0, may hold values from -4 to 4
- transport_v: float32 [256, 1024], P(('members', 'zonal'), 'merid'), parts along dimension 0, may hold values from -4 to 4
- thickness: float32 [14, 256, 1024], P(None, ('members', 'zonal'), 'merid'), parts along dimension 1, may hold values from 0.5 to 2
- velocity_u: float32 [14, 256, 1024], P(None, ('members', 'zonal'), 'merid'), parts along dimension 1, may hold values from -3 to 3
- velocity_v: float32 [14, 256, 1024], P(None, ('members', 'zonal'), 'merid'), parts along dimension 1, may hold values from -3 to 3
- sea_faces: int32 [2, 128, 1024], P(None, 'zonal', 'merid'), may hold values 0 or 1
- wind_seeds: int32 [8, 2], P('members'), parts along dimension 0, may hold values from 1 to 96
- wind_scale: float32 [8], P('members'), parts along dimension 0, may hold values from 0.5 to 2
- wind_base: float32 [2, 128, 1024], P(None, 'zonal', 'merid'), may hold values from -6 to 6
Outputs:
- final_height: float32 [256, 1024], P(('members', 'zonal'), 'merid'), parts along dimension 0
- final_transport_u: float32 [256, 1024], P(('members', 'zonal'), 'merid'), parts along dimension 0
- final_transport_v: float32 [256, 1024], P(('members', 'zonal'), 'merid'), parts along dimension 0
- final_thickness: float32 [14, 256, 1024], P(None, ('members', 'zonal'), 'merid'), parts along dimension 1
- final_velocity_u: float32 [14, 256, 1024], P(None, ('members', 'zonal'), 'merid'), parts along dimension 1
- final_velocity_v: float32 [14, 256, 1024], P(None, ('members', 'zonal'), 'merid'), parts along dimension 1
There are 2 independent parts, one for each index of `members`. A program takes and returns all parts, laid end to end along the dimension named above; an argument that names none is the same for every part. Nothing has to cross between parts.
All inputs are finite; a program needn't handle non-finite values. No bound on the sum of `sea_faces` on one device may be relied on, other than what follows from the above.
Results may differ from a plain program's by a relative error of at most 0.0001.
Values sent between devices are 32-bit elements; how exact they have to be, the bound alone decides.
No kernel may reach another device: no remote copies, remote signals or barrier semaphores. Data moves between devices by JAX's collectives and lax.ppermute only.
A program may use at most 64 MiB of HBM per device.

v0:
```python
import math

import jax
import jax.numpy as jnp
from jax import lax
from jax.sharding import PartitionSpec as P

NSUB = 6
STEPS = 2


WAVE_LIMIT = 0.225
STRESS_SCALE = 0.1
FLUX_STEP = 0.05
PRESS_COEF = 0.05


def extended(value, sides, width):
    for axis, dim in sides:
        devices, length = (lax.axis_size(axis), value.shape[dim])
        up = [(i, (i + 1) % devices) for i in range(devices)]
        down = [(j, i) for i, j in up]
        last = lax.slice_in_dim(value, length - width, length, axis=dim)
        leading = lax.slice_in_dim(value, 0, width, axis=dim)
        before = lax.ppermute(last, axis, up)
        after = lax.ppermute(leading, axis, down)
        value = jnp.concatenate([before, value, after], axis=dim)
    return value


def perturb(columns, rows_idx, wind_seeds, wind_scale, total_x, total_y):
    wave_x = wind_seeds[:, 0]
    wave_y = wind_seeds[:, 1]
    phase = (wave_x[:, None, None] * columns[None, :, None] % total_x).astype(jnp.float32) / total_x
    phase = (
        phase
        + (wave_y[:, None, None] * rows_idx[None, None, :] % total_y).astype(jnp.float32) / total_y
    )
    angle = 2.0 * math.pi * phase
    amplitude = wind_scale[:, None, None]
    return (
        jnp.sum(amplitude * jnp.cos(angle), axis=0),
        jnp.sum(amplitude * jnp.sin(angle), axis=0),
    )


def mirror_layers(top_rows):
    zonal_cells = top_rows.shape[1]
    whole = lax.all_gather(top_rows, "zonal", axis=1, tiled=True)
    start = (lax.axis_size("zonal") - 1 - lax.axis_index("zonal")) * zonal_cells
    piece = lax.dynamic_slice_in_dim(whole, start, zonal_cells, 1)
    return jnp.flip(piece, 1)


def mirror_static(block):
    width = block.shape[1]
    whole = lax.all_gather(block, "zonal", axis=1, tiled=True)
    start = (lax.axis_size("zonal") - 1 - lax.axis_index("zonal")) * width
    piece = lax.dynamic_slice_in_dim(whole, start, width, 1)
    return piece


def mirror_state(block):
    width = block.shape[1]
    whole = lax.all_gather(block, "zonal", axis=1, tiled=True)
    start = (lax.axis_size("zonal") - 1 - lax.axis_index("zonal")) * width
    piece = lax.dynamic_slice_in_dim(whole, start, width, 1)
    return piece


def clear_south(padded, bottom):
    first = lax.broadcasted_iota(jnp.int32, (1, 1, padded.shape[2]), 2) == 0
    return jnp.where(jnp.logical_and(bottom, first), jnp.float32(0.0), padded)


def clear_below(padded, merid_cells, margin):
    rows_ext = (
        lax.axis_index("merid") * merid_cells
        - margin
        + lax.broadcasted_iota(jnp.int32, (1, 1, padded.shape[2]), 2)
    )
    return jnp.where(rows_ext < 0, jnp.float32(0.0), padded)


def put_fold(north_field, folded, top):
    merid_cells = north_field.shape[-1]
    last = (
        lax.broadcasted_iota(jnp.int32, north_field.shape, north_field.ndim - 1) == merid_cells - 1
    )
    return jnp.where(jnp.logical_and(top, last), folded[..., None], north_field)


def from_low(field, axis):
    length = field.shape[axis]
    zero = jnp.zeros_like(lax.slice_in_dim(field, 0, 1, axis=axis))
    return jnp.concatenate([zero, lax.slice_in_dim(field, 0, length - 1, axis=axis)], axis=axis)


def from_high(field, axis):
    length = field.shape[axis]
    zero = jnp.zeros_like(lax.slice_in_dim(field, 0, 1, axis=axis))
    return jnp.concatenate([lax.slice_in_dim(field, 1, length, axis=axis), zero], axis=axis)


def advance_height(state):
    surface, flow_u, flow_v = state
    return surface - (flow_u - from_low(flow_u, 0) + flow_v - from_low(flow_v, 1))


def update_flows(surface, north_surf, state, statics):
    mask_u, mask_v, wave, stress_x, stress_y = statics
    flow_u = mask_u * (state[1] - wave * (from_high(surface, 0) - surface) + stress_x)
    flow_v = mask_v * (state[2] - wave * (north_surf - surface) + stress_y)
    return (surface, flow_u, flow_v)


def prepare_wide(mask_u, mask_v, wave, wind_base, wind_seeds, wind_scale, total_x, total_y):
    zonal_cells, merid_cells = wave.shape
    margin = NSUB + 1
    packed = jnp.stack([mask_u, mask_v, wave, wind_base[0], wind_base[1]])
    padded = extended(packed, (("zonal", 1), ("merid", 2)), margin)
    padded = clear_below(padded, merid_cells, margin)
    far = mirror_static(padded[:, :, merid_cells : merid_cells + margin])
    width = zonal_cells + 2 * margin
    spots = jnp.arange(width, dtype=jnp.int32)
    cols_own = (lax.axis_index("zonal") * zonal_cells - margin + spots) % total_x
    cols_far = (
        (lax.axis_size("zonal") - 1 - lax.axis_index("zonal")) * zonal_cells - margin + spots
    ) % total_x
    rows_own = (
        lax.axis_index("merid") * merid_cells
        - margin
        + jnp.arange(merid_cells + 2 * margin, dtype=jnp.int32)
    )
    rows_far = total_y - margin + jnp.arange(margin, dtype=jnp.int32)
    own_cos, own_sin = perturb(cols_own, rows_own, wind_seeds, wind_scale, total_x, total_y)
    far_cos, far_sin = perturb(cols_far, rows_far, wind_seeds, wind_scale, total_x, total_y)
    own = (
        padded[0],
        padded[1],
        padded[2],
        STRESS_SCALE * (padded[3] + own_cos),
        STRESS_SCALE * (padded[4] + own_sin),
    )
    mirrored = (
        far[0],
        far[1],
        far[2],
        STRESS_SCALE * (far[3] + far_cos),
        STRESS_SCALE * (far[4] + far_sin),
    )
    return (own, mirrored)


def interior(field, margin, zonal_cells, merid_cells):
    return field[margin : margin + zonal_cells, margin : margin + merid_cells]


def wide_substeps(surface, flow_u, flow_v, own, mirrored, top):
    zonal_cells, merid_cells = surface.shape
    margin = NSUB + 1
    packed = jnp.stack([surface, flow_u, flow_v])
    padded = extended(packed, (("zonal", 1), ("merid", 2)), margin)
    padded = clear_below(padded, merid_cells, margin)
    far = mirror_state(padded[:, :, merid_cells : merid_cells + margin])
    top_row = margin + merid_cells - 1
    row_ids = lax.broadcasted_iota(jnp.int32, padded.shape[1:], 1)
    fold_here = jnp.logical_and(top, row_ids == top_row)
    far_top = lax.broadcasted_iota(jnp.int32, far.shape[1:], 1) == margin - 1
    own_state = (padded[0], padded[1], padded[2])
    far_state = (far[0], far[1], far[2])
    sum_u = jnp.zeros_like(padded[1])
    sum_v = jnp.zeros_like(padded[2])
    for inner in range(NSUB):
        own_eta = advance_height(own_state)
        far_eta = advance_height(far_state)
        own_north = jnp.where(
            fold_here, jnp.flip(far_eta[:, margin - 1], 0)[:, None], from_high(own_eta, 1)
        )
        far_north = jnp.where(
            far_top, jnp.flip(own_eta[:, top_row], 0)[:, None], from_high(far_eta, 1)
        )
        own_state = update_flows(own_eta, own_north, own_state, own)
        far_state = update_flows(far_eta, far_north, far_state, mirrored)
        sum_u = sum_u + own_state[1]
        sum_v = sum_v + own_state[2]
    surface = interior(own_state[0], margin, zonal_cells, merid_cells)
    flow_u = interior(own_state[1], margin, zonal_cells, merid_cells)
    flow_v = interior(own_state[2], margin, zonal_cells, merid_cells)
    mean_u = interior(sum_u, margin, zonal_cells, merid_cells) / NSUB
    mean_v = interior(sum_v, margin, zonal_cells, merid_cells) / NSUB
    return (surface, flow_u, flow_v, mean_u, mean_v)


def layer_neighbours(thick, speed_u, speed_v, bottom, top):
    layers, zonal_cells, merid_cells = thick.shape
    folded = mirror_layers(thick[:, :, merid_cells - 1])
    packed = jnp.concatenate([thick, speed_u, speed_v], axis=0)
    padded = extended(packed, (("zonal", 1), ("merid", 2)), 1)
    padded = clear_south(padded, bottom)
    thick_pad = padded[:layers]
    west_u = padded[layers : 2 * layers, :zonal_cells, 1 : merid_cells + 1]
    south_v = padded[2 * layers :, 1 : zonal_cells + 1, :merid_cells]
    east_h = thick_pad[:, 2:, 1 : merid_cells + 1]
    west_h = thick_pad[:, :zonal_cells, 1 : merid_cells + 1]
    south_h = thick_pad[:, 1 : zonal_cells + 1, :merid_cells]
    north_h = put_fold(thick_pad[:, 1 : zonal_cells + 1, 2:], folded, top)
    return (east_h, west_h, south_h, north_h, west_u, south_v)


def body(
    height,
    transport_u,
    transport_v,
    thickness,
    velocity_u,
    velocity_v,
    sea_faces,
    wind_seeds,
    wind_scale,
    wind_base,
):
    zonal_cells, merid_cells = height.shape
    total_x = zonal_cells * lax.axis_size("zonal")
    total_y = merid_cells * lax.axis_size("merid")
    bottom = lax.axis_index("merid") == 0
    top = lax.axis_index("merid") == lax.axis_size("merid") - 1
    mask_u = sea_faces[0].astype(jnp.float32)
    mask_v = sea_faces[1].astype(jnp.float32)
    layers = thickness.shape[0]
    wave = WAVE_LIMIT / layers * jnp.sum(thickness, axis=0)
    own_static, far_static = prepare_wide(
        mask_u, mask_v, wave, wind_base, wind_seeds, wind_scale, total_x, total_y
    )
    surface, flow_u, flow_v = (height, transport_u, transport_v)
    thick, speed_u, speed_v = (thickness, velocity_u, velocity_v)
    depth_u = None
    depth_v = None
    for outer in range(STEPS):
        east_h, west_h, south_h, north_h, west_u, south_v = layer_neighbours(
            thick, speed_u, speed_v, bottom, top
        )
        thick_u = (thick + east_h) * 0.5
        thick_v = (thick + north_h) * 0.5
        if depth_u is None:
            depth_u = jnp.sum(thick_u, axis=0)
            depth_v = jnp.sum(thick_v, axis=0)
        surface, flow_u, flow_v, mean_u, mean_v = wide_substeps(
            surface, flow_u, flow_v, own_static, far_static, top
        )
        flux_u = speed_u * thick_u
        flux_v = speed_v * thick_v
        west_flux = west_u * (west_h + thick) * 0.5
        south_flux = south_v * (south_h + thick) * 0.5
        pressure = jnp.cumsum(thick, axis=0)
        east_press = jnp.cumsum(east_h, axis=0)
        north_press = jnp.cumsum(north_h, axis=0)
        trial_u = speed_u - PRESS_COEF * (east_press - pressure)
        trial_v = speed_v - PRESS_COEF * (north_press - pressure)
        speed_u = mask_u * (trial_u + (mean_u - jnp.sum(thick_u * trial_u, axis=0)) / depth_u)
        speed_v = mask_v * (trial_v + (mean_v - jnp.sum(thick_v * trial_v, axis=0)) / depth_v)
        thick = thick - FLUX_STEP * (flux_u - west_flux + flux_v - south_flux)
    return (surface, flow_u, flow_v, thick, speed_u, speed_v)


def solution(mesh):
    placed = (
        P(("members", "zonal"), "merid"),
        P(("members", "zonal"), "merid"),
        P(("members", "zonal"), "merid"),
        P(None, ("members", "zonal"), "merid"),
        P(None, ("members", "zonal"), "merid"),
        P(None, ("members", "zonal"), "merid"),
        P(None, "zonal", "merid"),
        P("members", None),
        P("members"),
        P(None, "zonal", "merid"),
    )
    return jax.shard_map(
        body,
        mesh=mesh,
        in_specs=placed,
        out_specs=(
            P(("members", "zonal"), "merid"),
            P(("members", "zonal"), "merid"),
            P(("members", "zonal"), "merid"),
            P(None, ("members", "zonal"), "merid"),
            P(None, ("members", "zonal"), "merid"),
            P(None, ("members", "zonal"), "merid"),
        ),
        check_vma=False,
    )
```

profile of v0, /device:TPU:1, one launch (start us, length us, event | category | flops | bytes accessed | tf_op | source)
XLA Modules:
  0.0 285.5 jit_solution(3082873381220074941)
XLA Ops:
  4.0 2.1 collective-permute-start.12
  6.0 3.0 %collective-permute-start.13 = (f32[42,1,512]{2,1,0:T(1,128)}, f32[42,1,512]{2,1,0:T(1,128)}, u32[]{:S(2)}, u32[]{:S(2)}) collective-permute-start(f32[42,1,512]{2,1,0:T(1,128)} %get-tuple-element.63), channel_id=1, source_target_pairs={{2,0},{4,2},{6,4},{8,6},{10,8},{12,10},{14,12},{0,14},{3,1},{5,3},... | collective-permute-start | bytes 258056 | tf_op jit(solution)/shard_map/ppermute | solution.py:26
  9.2 4.1 %collective-permute-start.1 = (f32[3,7,512]{2,1,0:T(8,128)S(1)}, f32[3,7,512]{2,1,0:T(8,128)S(1)}, u32[]{:S(2)}, u32[]{:S(2)}) collective-permute-start(f32[3,7,512]{2,1,0:T(8,128)S(1)} %get-tuple-element.111), channel_id=1, source_target_pairs={{2,0},{4,2},{6,4},{8,6},{10,8},{12,10},{14,12},{0,14},{3,1},{5,3},... | collective-permute-start | bytes 129032 | tf_op jit(solution)/shard_map/ppermute | solution.py:26
  13.4 2.2 fusion.143
  16.5 24.4 %all-gather = f32[14,128,1]{0,2,1:T(1,128)S(1)} all-gather(f32[14,16,1]{0,2,1:T(1,128)S(1)} %copy.262), channel_id=2, replica_groups=mesh['members'=2,'zonal'=8,'merid'=2] {'zonal'}, dimensions={1}, use_global_device_ids=true | all-gather | bytes 8064 | tf_op jit(solution)/shard_map/all_gather | solution.py:49
  42.8 3.6 %multiply_reduce_fusion.5 = (f32[30,526]{1,0:T(8,128)}, f32[30,526]{1,0:T(8,128)}) fusion(f32[4,526]{1,0:T(4,128)S(1)} %fusion.56, f32[4,30]{0,1:T(8,128)S(1)} %copy.207, f32[4]{0:T(128)S(1)} %copy-done.60), kind=kLoop, calls=%fused_computation.59 | loop fusion | flops 347160 | bytes 135152 | tf_op jit(solution)/shard_map/reduce_sum | solution.py:42
  46.5 7.7 %collective-permute-start.2 = (f32[3,30,7]{2,1,0:T(8,128)S(1)}, f32[3,30,7]{2,1,0:T(8,128)S(1)}, u32[]{:S(2)}, u32[]{:S(2)}) collective-permute-start(f32[3,30,7]{2,1,0:T(8,128)S(1)} %get-tuple-element.104), channel_id=1, source_target_pairs={{0,1},{1,0},{2,3},{3,2},{4,5},{5,4},{6,7},{7,6},{8,9},{9,8},{10,11... | collective-permute-start | bytes 7568 | tf_op jit(solution)/shard_map/ppermute | solution.py:25
  55.7 25.0 %all_gather.15 = f32[3,240,7]{2,0,1:T(4,128)S(1)} all-gather(f32[3,30,7]{2,0,1:T(4,128)S(1)} %copy.208), channel_id=1, replica_groups=mesh['members'=2,'zonal'=8,'merid'=2] {'zonal'}, dimensions={1}, use_global_device_ids=true | all-gather | bytes 22680 | tf_op jit(solution)/shard_map/all_gather | solution.py:65
  84.7 6.4 %collective-permute-start.14 = (f32[42,18,1]{2,0,1:T(8,128)}, f32[42,18,1]{2,0,1:T(8,128)}, u32[]{:S(2)}, u32[]{:S(2)}) collective-permute-start(f32[42,18,1]{2,0,1:T(8,128)} %get-tuple-element.59), channel_id=1, source_target_pairs={{0,1},{1,0},{2,3},{3,2},{4,5},{5,4},{6,7},{7,6},{8,9},{9,8},{10,11... | collective-permute-start | bytes 9080 | tf_op jit(solution)/shard_map/ppermute | solution.py:25
  93.9 1.9 pad_maximum_fusion
  97.6 2.9 %multiply_reduce_fusion.3 = (f32[16,512]{1,0:T(8,128)}, f32[16,512]{1,0:T(8,128)}, f32[16,512]{1,0:T(8,128)S(1)}, f32[16,512]{1,0:T(8,128)}, f32[16,512]{1,0:T(8...) fusion(f32[14,16,512]{2,1,0:T(8,128)S(1)} %copy-done, f32[42,18,514]{2,1,0:T(8,128)S(1)} %copy_select_fusion.1, ...), kind=kOutput, calls=%fused_computation.52 | output fusion | flops 4661248 | bytes 6595072 | tf_op jit(solution)/shard_map/jit(cumsum)/reduce_window_sum | solution.py:256
  100.6 4.1 %collective-permute-start.5 = (f32[5,7,512]{2,1,0:T(8,128)S(1)}, f32[5,7,512]{2,1,0:T(8,128)S(1)}, u32[]{:S(2)}, u32[]{:S(2)}) collective-permute-start(f32[5,7,512]{2,1,0:T(8,128)S(1)} %get-tuple-element.107), channel_id=1, source_target_pairs={{2,0},{4,2},{6,4},{8,6},{10,8},{12,10},{14,12},{0,14},{3,1},{5,3},... | collective-permute-start | bytes 215048 | tf_op jit(solution)/shard_map/ppermute | solution.py:26
  104.8 2.2 fusion.144
  107.3 24.2 %all-gather.1 = f32[14,128,1]{0,2,1:T(1,128)S(1)} all-gather(f32[14,16,1]{0,2,1:T(1,128)S(1)} %copy.232), channel_id=3, replica_groups=mesh['members'=2,'zonal'=8,'merid'=2] {'zonal'}, dimensions={1}, use_global_device_ids=true | all-gather | bytes 8064 | tf_op jit(solution)/shard_map/all_gather | solution.py:49
  131.7 7.4 %collective-permute-start.6 = (f32[5,30,7]{2,1,0:T(8,128)S(1)}, f32[5,30,7]{2,1,0:T(8,128)S(1)}, u32[]{:S(2)}, u32[]{:S(2)}) collective-permute-start(f32[5,30,7]{2,1,0:T(8,128)S(1)} %get-tuple-element.100), channel_id=1, source_target_pairs={{0,1},{1,0},{2,3},{3,2},{4,5},{5,4},{6,7},{7,6},{8,9},{9,8},{10,11... | collective-permute-start | bytes 12608 | tf_op jit(solution)/shard_map/ppermute | solution.py:25
  140.7 26.0 %all_gather.16 = f32[5,240,7]{2,0,1:T(8,128)S(1)} all-gather(f32[5,30,7]{2,0,1:T(8,128)S(1)} %copy.210), channel_id=1, replica_groups=mesh['members'=2,'zonal'=8,'merid'=2] {'zonal'}, dimensions={1}, use_global_device_ids=true | all-gather | bytes 37800 | tf_op jit(solution)/shard_map/all_gather | solution.py:57
  178.2 4.1 %collective-permute-start.9 = (f32[3,7,512]{2,1,0:T(8,128)S(1)}, f32[3,7,512]{2,1,0:T(8,128)S(1)}, u32[]{:S(2)}, u32[]{:S(2)}) collective-permute-start(f32[3,7,512]{2,1,0:T(8,128)S(1)} %get-tuple-element.109), channel_id=1, source_target_pairs={{2,0},{4,2},{6,4},{8,6},{10,8},{12,10},{14,12},{0,14},{3,1},{5,3},... | collective-permute-start | bytes 129032 | tf_op jit(solution)/shard_map/ppermute | solution.py:26
  184.4 7.7 %collective-permute-start.10 = (f32[3,30,7]{2,1,0:T(8,128)S(1)}, f32[3,30,7]{2,1,0:T(8,128)S(1)}, u32[]{:S(2)}, u32[]{:S(2)}) collective-permute-start(f32[3,30,7]{2,1,0:T(8,128)S(1)} %get-tuple-element.102), channel_id=1, source_target_pairs={{0,1},{1,0},{2,3},{3,2},{4,5},{5,4},{6,7},{7,6},{8,9},{9,8},{10,11... | collective-permute-start | bytes 7568 | tf_op jit(solution)/shard_map/ppermute | solution.py:25
  193.0 4.4 %collective-permute-start.17 = (f32[42,1,512]{2,1,0:T(1,128)}, f32[42,1,512]{2,1,0:T(1,128)}, u32[]{:S(2)}, u32[]{:S(2)}) collective-permute-start(f32[42,1,512]{2,1,0:T(1,128)} %get-tuple-element.61), channel_id=1, source_target_pairs={{2,0},{4,2},{6,4},{8,6},{10,8},{12,10},{14,12},{0,14},{3,1},{5,3},... | collective-permute-start | bytes 258056 | tf_op jit(solution)/shard_map/ppermute | solution.py:26
  199.1 25.7 %all_gather.17 = f32[3,240,7]{2,0,1:T(4,128)S(1)} all-gather(f32[3,30,7]{2,0,1:T(4,128)S(1)} %copy.212), channel_id=1, replica_groups=mesh['members'=2,'zonal'=8,'merid'=2] {'zonal'}, dimensions={1}, use_global_device_ids=true | all-gather | bytes 22680 | tf_op jit(solution)/shard_map/all_gather | solution.py:65
  267.7 6.6 %collective-permute-start.18 = (f32[42,18,1]{2,0,1:T(8,128)S(1)}, f32[42,18,1]{2,0,1:T(8,128)S(1)}, u32[]{:S(2)}, u32[]{:S(2)}) collective-permute-start(f32[42,18,1]{2,0,1:T(8,128)S(1)} %get-tuple-element.57), channel_id=1, source_target_pairs={{0,1},{1,0},{2,3},{3,2},{4,5},{5,4},{6,7},{7,6},{8,9},{9,8},{10,11... | collective-permute-start | bytes 9080 | tf_op jit(solution)/shard_map/ppermute | solution.py:25
  278.9 1.6 multiply_reduce_fusion
  280.5 1.7 fusion.46
  283.0 1.7 fusion.42
  (377 shorter events, 82.9 us)
Async XLA Ops:
  4.0 77.1 %collective-permute-start.12 = (f32[42,1,512]{2,1,0:T(1,128)S(1)}, f32[42,1,512]{2,1,0:T(1,128)}, u32[]{:S(2)}, u32[]{:S(2)}) collective-permute-start(f32[42,1,512]{2,1,0:T(1,128)S(1)} %get-tuple-element.64), channel_id=1, source_target_pairs={{0,2},{2,4},{4,6},{6,8},{8,10},{10,12},{12,14},{14,0},{1,3},{3,5},... | collective-permute-start | bytes 258056 | tf_op jit(solution)/shard_map/ppermute | solution.py:25
  6.0 76.7 %collective-permute-start.13 = (f32[42,1,512]{2,1,0:T(1,128)}, f32[42,1,512]{2,1,0:T(1,128)}, u32[]{:S(2)}, u32[]{:S(2)}) collective-permute-start(f32[42,1,512]{2,1,0:T(1,128)} %get-tuple-element.63), channel_id=1, source_target_pairs={{2,0},{4,2},{6,4},{8,6},{10,8},{12,10},{14,12},{0,14},{3,1},{5,3},... | collective-permute-start | bytes 258056 | tf_op jit(solution)/shard_map/ppermute | solution.py:26
  9.1 37.3 %collective-permute-start = (f32[3,7,512]{2,1,0:T(8,128)S(1)}, f32[3,7,512]{2,1,0:T(8,128)S(1)}, u32[]{:S(2)}, u32[]{:S(2)}) collective-permute-start(f32[3,7,512]{2,1,0:T(8,128)S(1)} %get-tuple-element.110), channel_id=1, source_target_pairs={{0,2},{2,4},{4,6},{6,8},{8,10},{10,12},{12,14},{14,0},{1,3},{3,5},... | collective-permute-start | bytes 129032 | tf_op jit(solution)/shard_map/ppermute | solution.py:25
  9.2 37.2 %collective-permute-start.1 = (f32[3,7,512]{2,1,0:T(8,128)S(1)}, f32[3,7,512]{2,1,0:T(8,128)S(1)}, u32[]{:S(2)}, u32[]{:S(2)}) collective-permute-start(f32[3,7,512]{2,1,0:T(8,128)S(1)} %get-tuple-element.111), channel_id=1, source_target_pairs={{2,0},{4,2},{6,4},{8,6},{10,8},{12,10},{14,12},{0,14},{3,1},{5,3},... | collective-permute-start | bytes 129032 | tf_op jit(solution)/shard_map/ppermute | solution.py:26
  15.7 65.3 %copy-start.51 = (pred[526]{0:T(1024)(128)(4,1)}, pred[526]{0:T(1024)(128)(4,1)S(1)}, u32[]{:S(2)}) copy-start(pred[526]{0:T(1024)(128)(4,1)S(1)} %broadcast_compare_fusion) | copy-start | bytes 1582
  46.5 8.6 %collective-permute-start.2 = (f32[3,30,7]{2,1,0:T(8,128)S(1)}, f32[3,30,7]{2,1,0:T(8,128)S(1)}, u32[]{:S(2)}, u32[]{:S(2)}) collective-permute-start(f32[3,30,7]{2,1,0:T(8,128)S(1)} %get-tuple-element.104), channel_id=1, source_target_pairs={{0,1},{1,0},{2,3},{3,2},{4,5},{5,4},{6,7},{7,6},{8,9},{9,8},{10,11... | collective-permute-start | bytes 7568 | tf_op jit(solution)/shard_map/ppermute | solution.py:25
  54.2 1.2 collective-permute-start.3
  84.7 9.2 %collective-permute-start.14 = (f32[42,18,1]{2,0,1:T(8,128)}, f32[42,18,1]{2,0,1:T(8,128)}, u32[]{:S(2)}, u32[]{:S(2)}) collective-permute-start(f32[42,18,1]{2,0,1:T(8,128)} %get-tuple-element.59), channel_id=1, source_target_pairs={{0,1},{1,0},{2,3},{3,2},{4,5},{5,4},{6,7},{7,6},{8,9},{9,8},{10,11... | collective-permute-start | bytes 9080 | tf_op jit(solution)/shard_map/ppermute | solution.py:25
  91.1 2.7 collective-permute-start.15
  100.6 31.0 %collective-permute-start.4 = (f32[5,7,512]{2,1,0:T(8,128)S(1)}, f32[5,7,512]{2,1,0:T(8,128)S(1)}, u32[]{:S(2)}, u32[]{:S(2)}) collective-permute-start(f32[5,7,512]{2,1,0:T(8,128)S(1)} %get-tuple-element.106), channel_id=1, source_target_pairs={{0,2},{2,4},{4,6},{6,8},{8,10},{10,12},{12,14},{14,0},{1,3},{3,5},... | collective-permute-start | bytes 215048 | tf_op jit(solution)/shard_map/ppermute | solution.py:25
  100.6 30.9 %collective-permute-start.5 = (f32[5,7,512]{2,1,0:T(8,128)S(1)}, f32[5,7,512]{2,1,0:T(8,128)S(1)}, u32[]{:S(2)}, u32[]{:S(2)}) collective-permute-start(f32[5,7,512]{2,1,0:T(8,128)S(1)} %get-tuple-element.107), channel_id=1, source_target_pairs={{2,0},{4,2},{6,4},{8,6},{10,8},{12,10},{14,12},{0,14},{3,1},{5,3},... | collective-permute-start | bytes 215048 | tf_op jit(solution)/shard_map/ppermute | solution.py:26
  107.1 61.6 %copy-start.45 = (pred[7]{0:T(512)(128)(4,1)S(1)}, pred[7]{0:T(512)(128)(4,1)}, u32[]{:S(2)}) copy-start(pred[7]{0:T(512)(128)(4,1)} %iota_compare_fusion.3) | copy-start | bytes 25
  107.1 61.6 %copy-start.48 = (f32[30,7]{0,1:T(8,128)S(1)}, f32[30,7]{0,1:T(8,128)}, u32[]{:S(2)}) copy-start(f32[30,7]{0,1:T(8,128)} %get-tuple-element.41) | copy-start | bytes 2524
  107.1 61.6 %copy-start.49 = (f32[30,7]{0,1:T(8,128)S(1)}, f32[30,7]{0,1:T(8,128)}, u32[]{:S(2)}) copy-start(f32[30,7]{0,1:T(8,128)} %get-tuple-element.42) | copy-start | bytes 2524
  131.7 8.3 %collective-permute-start.6 = (f32[5,30,7]{2,1,0:T(8,128)S(1)}, f32[5,30,7]{2,1,0:T(8,128)S(1)}, u32[]{:S(2)}, u32[]{:S(2)}) collective-permute-start(f32[5,30,7]{2,1,0:T(8,128)S(1)} %get-tuple-element.100), channel_id=1, source_target_pairs={{0,1},{1,0},{2,3},{3,2},{4,5},{5,4},{6,7},{7,6},{8,9},{9,8},{10,11... | collective-permute-start | bytes 12608 | tf_op jit(solution)/shard_map/ppermute | solution.py:25
  139.1 1.3 collective-permute-start.7
  178.1 6.1 %collective-permute-start.8 = (f32[3,7,512]{2,1,0:T(8,128)S(1)}, f32[3,7,512]{2,1,0:T(8,128)S(1)}, u32[]{:S(2)}, u32[]{:S(2)}) collective-permute-start(f32[3,7,512]{2,1,0:T(8,128)S(1)} %get-tuple-element.108), channel_id=1, source_target_pairs={{0,2},{2,4},{4,6},{6,8},{8,10},{10,12},{12,14},{14,0},{1,3},{3,5},... | collective-permute-start | bytes 129032 | tf_op jit(solution)/shard_map/ppermute | solution.py:25
  178.2 6.1 %collective-permute-start.9 = (f32[3,7,512]{2,1,0:T(8,128)S(1)}, f32[3,7,512]{2,1,0:T(8,128)S(1)}, u32[]{:S(2)}, u32[]{:S(2)}) collective-permute-start(f32[3,7,512]{2,1,0:T(8,128)S(1)} %get-tuple-element.109), channel_id=1, source_target_pairs={{2,0},{4,2},{6,4},{8,6},{10,8},{12,10},{14,12},{0,14},{3,1},{5,3},... | collective-permute-start | bytes 129032 | tf_op jit(solution)/shard_map/ppermute | solution.py:26
  184.4 13.0 %collective-permute-start.10 = (f32[3,30,7]{2,1,0:T(8,128)S(1)}, f32[3,30,7]{2,1,0:T(8,128)S(1)}, u32[]{:S(2)}, u32[]{:S(2)}) collective-permute-start(f32[3,30,7]{2,1,0:T(8,128)S(1)} %get-tuple-element.102), channel_id=1, source_target_pairs={{0,1},{1,0},{2,3},{3,2},{4,5},{5,4},{6,7},{7,6},{8,9},{9,8},{10,11... | collective-permute-start | bytes 7568 | tf_op jit(solution)/shard_map/ppermute | solution.py:25
  192.1 5.3 %collective-permute-start.11 = (f32[3,30,7]{2,1,0:T(8,128)S(1)}, f32[3,30,7]{2,1,0:T(8,128)S(1)}, u32[]{:S(2)}, u32[]{:S(2)}) collective-permute-start(f32[3,30,7]{2,1,0:T(8,128)S(1)} %get-tuple-element.103), channel_id=1, source_target_pairs={{1,0},{0,1},{3,2},{2,3},{5,4},{4,5},{7,6},{6,7},{9,8},{8,9},{11,10... | collective-permute-start | bytes 7568 | tf_op jit(solution)/shard_map/ppermute | solution.py:26
  193.0 71.9 %collective-permute-start.16 = (f32[42,1,512]{2,1,0:T(1,128)}, f32[42,1,512]{2,1,0:T(1,128)}, u32[]{:S(2)}, u32[]{:S(2)}) collective-permute-start(f32[42,1,512]{2,1,0:T(1,128)} %get-tuple-element.62), channel_id=1, source_target_pairs={{0,2},{2,4},{4,6},{6,8},{8,10},{10,12},{12,14},{14,0},{1,3},{3,5},... | collective-permute-start | bytes 258056 | tf_op jit(solution)/shard_map/ppermute | solution.py:25
  193.0 73.7 %collective-permute-start.17 = (f32[42,1,512]{2,1,0:T(1,128)}, f32[42,1,512]{2,1,0:T(1,128)}, u32[]{:S(2)}, u32[]{:S(2)}) collective-permute-start(f32[42,1,512]{2,1,0:T(1,128)} %get-tuple-element.61), channel_id=1, source_target_pairs={{2,0},{4,2},{6,4},{8,6},{10,8},{12,10},{14,12},{0,14},{3,1},{5,3},... | collective-permute-start | bytes 258056 | tf_op jit(solution)/shard_map/ppermute | solution.py:26
  267.7 8.0 %collective-permute-start.18 = (f32[42,18,1]{2,0,1:T(8,128)S(1)}, f32[42,18,1]{2,0,1:T(8,128)S(1)}, u32[]{:S(2)}, u32[]{:S(2)}) collective-permute-start(f32[42,18,1]{2,0,1:T(8,128)S(1)} %get-tuple-element.57), channel_id=1, source_target_pairs={{0,1},{1,0},{2,3},{3,2},{4,5},{5,4},{6,7},{7,6},{8,9},{9,8},{10,11... | collective-permute-start | bytes 9080 | tf_op jit(solution)/shard_map/ppermute | solution.py:25
  274.3 2.1 collective-permute-start.19
  (57 other events, 639.1 us)
where the time goes:
time: 288 us; the launch traced here: 285 us
  blocking collectives  125 us (43%)
  starting transfers between devices  58.3 us (20%)
  local copies, waits for them, and re-layouts  52 us (18%)
  other arithmetic  46 us (16%)
    all_gather x2, blocking collectives, mirror_state(): whole = lax.all_gather(block, 'zonal', axis=1, tiled=True)  50.7 us
    all_gather x2, blocking collectives, mirror_layers(): whole = lax.all_gather(top_rows, 'zonal', axis=1, tiled=True)  48.7 us
    ppermute x10, starting transfers between devices, extended(): before = lax.ppermute(last, axis, up)  38 us
    all_gather x1, blocking collectives, mirror_static(): whole = lax.all_gather(block, 'zonal', axis=1, tiled=True)  26 us
    ppermute x10, starting transfers between devices, extended(): after = lax.ppermute(leading, axis, down)  20.2 us
    slice x44, local copies, waits for them, and re-layouts, from_high(): lax.slice_in_dim(field, 1, length, axis=axis)  15.4 us
    unnamed x144, local copies, waits for them, and re-layouts  12.2 us
    mul x21, other arithmetic, update_flows(): mask_u * (state[1] - wave * (from_high(surface, 0) - surface) + stress_x)  12.1 us
  transfers between devices with their start and end apart: 20, of which 6 were waited for; matrix products, arithmetic and copies ran while one was open for 22% of the time, Pallas kernels for 0%

commit v1 on v0

v1 whole, which is shorter than its diff:
```python
import math

import jax
import jax.numpy as jnp
from jax import lax
from jax.experimental import pallas as pl
from jax.experimental.pallas import tpu as pltpu
from jax.sharding import PartitionSpec as P

NSUB = 6
STEPS = 2
WAVE_LIMIT = 0.225
STRESS_SCALE = 0.1
FLUX_STEP = 0.05
PRESS_COEF = 0.05

FIELDS = 8
HALO = NSUB * STEPS
SLOT = 16
LANES = 128
EDGE = 8

VMEM = pl.BlockSpec(memory_space=pltpu.VMEM)
SMEM = pl.BlockSpec(memory_space=pltpu.SMEM)


def whole_mod(product, total):
    rest = product - jnp.floor(product * (1.0 / total)) * total
    rest = jnp.where(rest < 0.0, rest + total, rest)
    return jnp.where(rest >= total, rest - total, rest)


def east_rows(layers):
    return FIELDS * HALO + 4 * layers


def west_rows(layers):
    return FIELDS * HALO + 5 * layers


def prepare_kernel(total_x, total_y, place, seeds, scale, eta, bu, bv, thick, vu, vv, faces, base, fields, to_west, to_east):
    layers, rows, cols = thick.shape
    modes = scale.shape[0]
    f32 = jnp.float32

    lane = lax.broadcasted_iota(jnp.int32, (rows, LANES), 1)
    sub = lax.broadcasted_iota(jnp.int32, (8, cols), 0)
    wave_x = jnp.zeros((rows, LANES), f32)
    wave_y = jnp.zeros((8, cols), f32)
    for m in range(modes):
        wave_x = jnp.where(lane == m, seeds[m, 0].astype(f32), wave_x)
        wave_y = jnp.where(sub == m, seeds[m, 1].astype(f32), wave_y)
    col = (lax.broadcasted_iota(jnp.int32, (rows, LANES), 0) + place[0] * rows).astype(f32)
    row = (lax.broadcasted_iota(jnp.int32, (8, cols), 1) + place[1] * cols).astype(f32)
    angle_x = whole_mod(wave_x * col, total_x) * (2.0 * math.pi / total_x)
    angle_y = whole_mod(wave_y * row, total_y) * (2.0 * math.pi / total_y)
    cos_x, sin_x = jnp.cos(angle_x), jnp.sin(angle_x)
    cos_y, sin_y = jnp.cos(angle_y), jnp.sin(angle_y)
    sum_cos = base[0]
    sum_sin = base[1]
    for m in range(modes):
        amp = scale[m]
        ca = cos_x[:, m : m + 1] * amp
        sa = sin_x[:, m : m + 1] * amp
        cb = cos_y[m : m + 1, :]
        sb = sin_y[m : m + 1, :]
        sum_cos = sum_cos + (ca * cb - sa * sb)
        sum_sin = sum_sin + (sa * cb + ca * sb)
    fields[0] = eta[...]
    fields[1] = bu[...]
    fields[2] = bv[...]
    total = thick[0]
    for k in range(1, layers):
        total = total + thick[k]
    fields[3] = total
    fields[4] = faces[0].astype(f32)
    fields[5] = faces[1].astype(f32)
    fields[6] = STRESS_SCALE * sum_cos
    fields[7] = STRESS_SCALE * sum_sin
    for f in range(FIELDS):
        value = fields[f]
        to_west[f * HALO : (f + 1) * HALO, :] = value[:HALO]
        to_east[f * HALO : (f + 1) * HALO, :] = value[rows - HALO :]
    at = FIELDS * HALO
    for k in range(layers):
        to_west[at + 2 * k : at + 2 * k + 2, :] = thick[k, 0:2, :]
        to_east[at + 2 * k : at + 2 * k + 2, :] = thick[k, rows - 2 : rows, :]
        to_west[at + 2 * layers + k : at + 2 * layers + k + 1, :] = vu[k, 0:1, :]
        to_west[at + 3 * layers + k : at + 3 * layers + k + 1, :] = vv[k, 0:1, :]
        to_east[at + 2 * layers + 2 * k : at + 2 * layers + 2 * k + 2, :] = vu[k, rows - 2 : rows, :]
        to_east[at + 4 * layers + k : at + 4 * layers + k + 1, :] = vv[k, rows - 1 : rows, :]


def fill_fields(target, f, fields, east, west, rows):
    cols = fields.shape[-1]
    target[f, 0:rows, 0:cols] = fields[f]
    target[f, rows : rows + HALO, 0:cols] = east[f * HALO : (f + 1) * HALO, :]
    target[f, rows + HALO : rows + 2 * HALO, 0:cols] = west[f * HALO : (f + 1) * HALO, :]


def fill_layers(target, k, layers, thick, vu, vv, east, west, rows):
    cols = thick.shape[-1]
    at = FIELDS * HALO
    e, w = rows, rows + EDGE
    zero = jnp.zeros((EDGE, cols), jnp.float32)
    for s, own in enumerate((thick, vu, vv)):
        target[s * layers + k, 0:rows, 0:cols] = own[k]
        target[s * layers + k, rows : rows + EDGE, 0:cols] = zero
    target[k, e : e + 2, 0:cols] = east[at + 2 * k : at + 2 * k + 2, :]
    target[k, w - 2 : w, 0:cols] = west[at + 2 * k : at + 2 * k + 2, :]
    target[layers + k, e : e + 1, 0:cols] = east[at + 2 * layers + k : at + 2 * layers + k + 1, :]
    target[layers + k, w - 2 : w, 0:cols] = west[at + 2 * layers + 2 * k : at + 2 * layers + 2 * k + 2, :]
    target[2 * layers + k, e : e + 1, 0:cols] = east[at + 3 * layers + k : at + 3 * layers + k + 1, :]
    target[2 * layers + k, w - 1 : w, 0:cols] = west[at + 4 * layers + k : at + 4 * layers + k + 1, :]


def flipped(pack, rows, group):
    size = pack.shape[0]
    q = lax.broadcasted_iota(jnp.int32, (size, size), 0)
    p = lax.broadcasted_iota(jnp.int32, (size, size), 1)
    source = rows - 1 - q
    source = jnp.where(source < 0, source + size, source)
    flip_rows = (p == source).astype(jnp.float32)
    a = lax.broadcasted_iota(jnp.int32, (LANES, LANES), 0)
    b = lax.broadcasted_iota(jnp.int32, (LANES, LANES), 1)
    inner = jnp.bitwise_and(b, group - 1)
    flip_lanes = (a == b - inner + (group - 1 - inner)).astype(jnp.float32)
    half = jnp.dot(flip_rows, pack, precision=lax.Precision.HIGHEST, preferred_element_type=jnp.float32)
    return jnp.dot(half, flip_lanes, precision=lax.Precision.HIGHEST, preferred_element_type=jnp.float32)


def pack_kernel(
    place,
    fields_a, thick_a, vu_a, vv_a, east_a, west_a,
    fields_b, thick_b, vu_b, vv_b, east_b, west_b,
    low, high, fold, wide, deep,
):
    layers, rows, _ = thick_a.shape
    tall = rows + 2 * HALO
    short = rows + EDGE
    lane_f = lax.broadcasted_iota(jnp.int32, (tall, LANES), 1)
    lane_l = lax.broadcasted_iota(jnp.int32, (short, LANES), 1)
    sides = (
        (low, 0, SLOT, fields_a, thick_a, vu_a, vv_a, east_a, west_a),
        (high, LANES - SLOT, LANES - 2, fields_b, thick_b, vu_b, vv_b, east_b, west_b),
    )
    for out, start, _, fields, thick, vu, vv, east, west in sides:
        first = 0 if start == 0 else LANES - 2
        acc = jnp.zeros((tall, LANES), jnp.float32)
        for f in range(FIELDS):
            fill_fields(wide, f, fields, east, west, rows)
            moved = pltpu.roll(wide[f], (f * SLOT - start) % LANES, 1)
            acc = jnp.where(lane_f // SLOT == f, moved, acc)
        out[0:tall, :] = acc
        acc_l = jnp.zeros((short, LANES), jnp.float32)
        for k in range(layers):
            fill_layers(deep, k, layers, thick, vu, vv, east, west, rows)
        for k in range(3 * layers):
            moved = pltpu.roll(deep[k], (2 * k - first) % LANES, 1)
            acc_l = jnp.where(lane_l // 2 == k, moved, acc_l)
        out[tall : tall + short, :] = acc_l
        if start != 0:
            fold[0:tall, :] = flipped(acc, rows, SLOT)
            fold[tall : tall + short, :] = flipped(acc_l, rows, 2)


def make_neighbours(ghost, cols):
    def east(a):
        n = a.shape[0]
        g = ghost[n]
        plus = pltpu.roll(a, n - 1, 0)
        return jnp.concatenate(
            [plus[:, :cols], jnp.where(g, pltpu.roll(a[:, cols:], 1, 0), plus[:, cols:])], axis=1
        )

    def west(a):
        n = a.shape[0]
        g = ghost[n]
        minus = pltpu.roll(a, 1, 0)
        return jnp.concatenate(
            [minus[:, :cols], jnp.where(g, pltpu.roll(a[:, cols:], n - 1, 0), minus[:, cols:])], axis=1
        )

    def north(a):
        g = ghost[a.shape[0]]
        plus = pltpu.roll(a, cols + LANES - 1, 1)
        minus = pltpu.roll(a[:, cols - LANES :], 1, 1)[:, LANES:]
        return jnp.concatenate([plus[:, :cols], jnp.where(g, minus, plus[:, cols:])], axis=1)

    def south(a):
        g = ghost[a.shape[0]]
        minus = pltpu.roll(a, 1, 1)
        plus = pltpu.roll(a[:, cols:], LANES - 1, 1)
        return jnp.concatenate([minus[:, :cols], jnp.where(g, plus, minus[:, cols:])], axis=1)

    return east, west, north, south


def main_kernel(
    place, fields, thick, vu, vv, east_in, west_in, north_in, south_in,
    out_eta, out_bu, out_bv, out_h, out_u, out_v, wide, deep,
):
    layers, rows, cols = thick.shape
    tall = rows + 2 * HALO
    short = rows + EDGE
    top = place[2] == 1
    bottom = place[3] == 1
    lanes = {n: lax.broadcasted_iota(jnp.int32, (n, LANES), 1) for n in (tall, short)}
    ghost = {n: jnp.logical_and(top, lanes[n] < LANES // 2) for n in (tall, short)}
    east, west, north, south = make_neighbours(ghost, cols)

    pack_n = north_in[0:tall, :]
    pack_s = jnp.where(bottom, 0.0, south_in[0:tall, :])
    for f in range(FIELDS):
        fill_fields(wide, f, fields, east_in, west_in, rows)
        up = pltpu.roll(pack_n, (-f * SLOT) % LANES, 1)
        down = pltpu.roll(pack_s, (LANES - SLOT - f * SLOT) % LANES, 1)
        edge = jnp.where(lanes[tall] >= LANES - SLOT, down, 0.0)
        wide[f, :, cols:] = jnp.where(lanes[tall] < SLOT, up, edge)
    deep_n = north_in[tall : tall + short, :]
    deep_s = jnp.where(bottom, 0.0, south_in[tall : tall + short, :])
    for k in range(layers):
        fill_layers(deep, k, layers, thick, vu, vv, east_in, west_in, rows)
    for k in range(3 * layers):
        up = pltpu.roll(deep_n, (-2 * k) % LANES, 1)
        down = pltpu.roll(deep_s, (LANES - 2 - 2 * k) % LANES, 1)
        edge = jnp.where(lanes[short] >= LANES - 2, down, 0.0)
        deep[k, :, cols:] = jnp.where(lanes[short] < 2, up, edge)

    near = lax.broadcasted_iota(jnp.int32, (EDGE, cols + LANES), 0) < EDGE // 2

    def shorten(a):
        return jnp.concatenate([a[:rows], jnp.where(near, a[rows : rows + EDGE], a[tall - EDGE :])], axis=0)

    total = wide[3]
    wave = (WAVE_LIMIT / layers) * total
    total_short = shorten(total)
    depth_u = (total_short + east(total_short)) * 0.5
    depth_v = (total_short + north(total_short)) * 0.5
    depth_u = 1.0 / jnp.where(depth_u > 0.0, depth_u, 1.0)
    depth_v = 1.0 / jnp.where(depth_v > 0.0, depth_v, 1.0)
    mask_u = wide[4]
    mask_v = wide[5]
    short_mask_u = shorten(mask_u)
    short_mask_v = shorten(mask_v)
    stress_x = wide[6]
    stress_y = wide[7]
    eta = wide[0]
    bu = wide[1]
    bv = wide[2]
    for step in range(STEPS):
        sum_u = jnp.zeros_like(bu)
        sum_v = jnp.zeros_like(bv)
        for _ in range(NSUB):
            eta = eta - (bu - west(bu) + bv - south(bv))
            bu = mask_u * (bu - wave * (east(eta) - eta) + stress_x)
            bv = mask_v * (bv - wave * (north(eta) - eta) + stress_y)
            sum_u = sum_u + bu
            sum_v = sum_v + bv
        mean_u = shorten(sum_u) * (1.0 / NSUB)
        mean_v = shorten(sum_v) * (1.0 / NSUB)
        last = step == STEPS - 1

        def first_pass(k, carry):
            press_u, press_v, total_u, total_v = carry
            h = deep[k]
            u = deep[layers + k]
            v = deep[2 * layers + k]
            east_h = east(h)
            north_h = north(h)
            thick_u = (h + east_h) * 0.5
            thick_v = (h + north_h) * 0.5
            press_u = press_u + (east_h - h)
            press_v = press_v + (north_h - h)
            trial_u = u - PRESS_COEF * press_u
            trial_v = v - PRESS_COEF * press_v
            flux_u = u * thick_u
            flux_v = v * thick_v
            new = h - FLUX_STEP * (flux_u - west(flux_u) + flux_v - south(flux_v))
            if last:
                out_h[k] = new[:rows, :cols]
            else:
                deep[k] = new
            deep[layers + k] = trial_u
            deep[2 * layers + k] = trial_v
            return press_u, press_v, total_u + thick_u * trial_u, total_v + thick_v * trial_v

        zero = jnp.zeros((short, cols + LANES), jnp.float32)
        _, _, total_u, total_v = lax.fori_loop(0, layers, first_pass, (zero, zero, zero, zero))
        fix_u = (mean_u - total_u) * depth_u
        fix_v = (mean_v - total_v) * depth_v

        def second_pass(k, carry):
            new_u = short_mask_u * (deep[layers + k] + fix_u)
            new_v = short_mask_v * (deep[2 * layers + k] + fix_v)
            if last:
                out_u[k] = new_u[:rows, :cols]
                out_v[k] = new_v[:rows, :cols]
            else:
                deep[layers + k] = new_u
                deep[2 * layers + k] = new_v
            return carry

        lax.fori_loop(0, layers, second_pass, 0)
    out_eta[...] = eta[:rows, :cols]
    out_bu[...] = bu[:rows, :cols]
    out_bv[...] = bv[:rows, :cols]


def body(
    height,
    transport_u,
    transport_v,
    thickness,
    velocity_u,
    velocity_v,
    sea_faces,
    wind_seeds,
    wind_scale,
    wind_base,
):
    layers, rows, cols = thickness.shape
    f32 = jnp.float32
    zonal = lax.axis_size("zonal")
    merid = lax.axis_size("merid")
    z = lax.axis_index("zonal")
    m = lax.axis_index("merid")
    tall = rows + 2 * HALO
    short = rows + EDGE
    place = jnp.stack([z, m, (m == merid - 1).astype(jnp.int32), (m == 0).astype(jnp.int32)]).astype(jnp.int32)

    fields, to_west, to_east = pl.pallas_call(
        lambda *refs: prepare_kernel(rows * zonal, cols * merid, *refs),
        out_shape=(
            jax.ShapeDtypeStruct((FIELDS, rows, cols), f32),
            jax.ShapeDtypeStruct((east_rows(layers), cols), f32),
            jax.ShapeDtypeStruct((west_rows(layers), cols), f32),
        ),
        in_specs=[SMEM, SMEM, SMEM] + [VMEM] * 8,
        out_specs=(VMEM, VMEM, VMEM),
        name="prepare",
    )(place, wind_seeds, wind_scale, height, transport_u, transport_v, thickness, velocity_u, velocity_v, sea_faces, wind_base)

    up = [(i, (i + 1) % zonal) for i in range(zonal)]
    down = [(j, i) for i, j in up]
    east = lax.ppermute(to_west, "zonal", down)
    west = lax.ppermute(to_east, "zonal", up)

    tile_last = cols // LANES - 1
    edge_inputs = (fields, thickness, velocity_u, velocity_v, east, west)

    def edge_specs(tile):
        return [
            pl.BlockSpec(a.shape[:-1] + (LANES,), lambda i, n=a.ndim: (0,) * (n - 1) + (tile,)) for a in edge_inputs
        ]

    pack_shape = jax.ShapeDtypeStruct((tall + short, LANES), f32)
    low, high, fold = pl.pallas_call(
        pack_kernel,
        grid=(1,),
        out_shape=(pack_shape, pack_shape, pack_shape),
        in_specs=[SMEM] + edge_specs(0) + edge_specs(tile_last),
        out_specs=(pl.BlockSpec((tall + short, LANES), lambda i: (0, 0)),) * 3,
        scratch_shapes=[
            pltpu.VMEM((FIELDS, tall, LANES), f32),
            pltpu.VMEM((3 * layers, short, LANES), f32),
        ],
        name="pack",
    )(place, *edge_inputs, *edge_inputs)

    mirror = [(i * merid + merid - 1, (zonal - 1 - i) * merid + merid - 1) for i in range(zonal)]
    folded = lax.ppermute(fold, ("zonal", "merid"), mirror)
    if merid == 2:
        swapped = lax.ppermute(jnp.where(m == 0, high, low), "merid", [(0, 1), (1, 0)])
        from_north = swapped
        from_south = swapped
    else:
        from_north = lax.ppermute(low, "merid", [(i + 1, i) for i in range(merid - 1)])
        from_south = lax.ppermute(high, "merid", [(i, i + 1) for i in range(merid - 1)])
    from_north = jnp.where(m == merid - 1, folded, from_north)

    flat = jax.ShapeDtypeStruct((rows, cols), f32)
    full = jax.ShapeDtypeStruct((layers, rows, cols), f32)
    return pl.pallas_call(
        main_kernel,
        out_shape=(flat, flat, flat, full, full, full),
        in_specs=[SMEM] + [VMEM] * 8,
        out_specs=(VMEM,) * 6,
        scratch_shapes=[
            pltpu.VMEM((FIELDS, tall, cols + LANES), f32),
            pltpu.VMEM((3 * layers, short, cols + LANES), f32),
        ],
        name="advance",
    )(place, fields, thickness, velocity_u, velocity_v, east, west, from_north, from_south)


def solution(mesh):
    placed = (
        P(("members", "zonal"), "merid"),
        P(("members", "zonal"), "merid"),
        P(("members", "zonal"), "merid"),
        P(None, ("members", "zonal"), "merid"),
        P(None, ("members", "zonal"), "merid"),
        P(None, ("members", "zonal"), "merid"),
        P(None, "zonal", "merid"),
        P("members", None),
        P("members"),
        P(None, "zonal", "merid"),
    )
    return jax.shard_map(
        body,
        mesh=mesh,
        in_specs=placed,
        out_specs=(
            P(("members", "zonal"), "merid"),
            P(("members", "zonal"), "merid"),
            P(("members", "zonal"), "merid"),
            P(None, ("members", "zonal"), "merid"),
            P(None, ("members", "zonal"), "merid"),
            P(None, ("members", "zonal"), "merid"),
        ),
        check_vma=False,
    )
```

time: 288 us -> 47.5 us (0.16)
  blocking collectives: 125 us -> 0 us
  local copies, waits for them, and re-layouts: 52 us -> 2.17 us
  starting transfers between devices: 58.3 us -> 11.7 us
  other arithmetic: 46 us -> 2.01 us
  Pallas kernels: 0 us -> 15.6 us
  waiting for transfers between devices: 2.16 us -> 15 us
    all_gather x5 -> x0, blocking collectives: 125 us -> none  [the longest x2 50.7 us: mirror_state(): whole = lax.all_gather(block, 'zonal', axis=1, tiled=True)]
    ppermute x20 -> x4, starting transfers between devices: 58.3 us -> 11.7 us  [the longest x1 4.83 us: body(): folded = lax.ppermute(fold, ('zonal', 'merid'), mirror)]
    slice x78 -> x0, local copies, waits for them, and re-layouts: 24.2 us -> none  [the longest x44 15.4 us: from_high(): lax.slice_in_dim(field, 1, length, axis=axis)]
    mul x28 -> x0, other arithmetic: 16.1 us -> none  [the longest x21 12.1 us: update_flows(): mask_u * (state[1] - wave * (from_high(surface, 0) - surface) + stress_x)]
    pallas_call x0 -> x3, Pallas kernels: none -> 15.6 us  [the longest x1 10.6 us: body(): pl.pallas_call(main_kernel, out_shape=(flat, flat, flat, full, full, full...]
    ppermute x20 -> x4, waiting for transfers between devices: 2.16 us -> 15 us  [the longest x1 12.5 us: body(): east = lax.ppermute(to_west, 'zonal', down)]
    unnamed x144 -> x11, local copies, waits for them, and re-layouts: 12.2 us -> 2.17 us
    rev x24 -> x0, local copies, waits for them, and re-layouts: 8.98 us -> none  [the longest x12 6.69 us: wide_substeps(): jnp.flip(far_eta[:, margin - 1], 0)[:, None]]
  transfers between devices with their start and end apart: 20 -> 4, of which waited for: 6 -> 2; matrix products, arithmetic and copies ran while one was open for 22% -> 0% of each run, Pallas kernels for 0% -> 0%
where the time goes in v1:
time: 47.5 us; the launch traced here: 47.2 us
  Pallas kernels  15.6 us (33%)
  waiting for transfers between devices  15 us (32%)
  starting transfers between devices  11.7 us (25%)
  local copies, waits for them, and re-layouts  2.17 us (5%)
  other arithmetic  2.01 us (4%)
  between operations  0.68 us (1%)
    ppermute x1, waiting for transfers between devices, body(): east = lax.ppermute(to_west, 'zonal', down)  12.5 us
    pallas_call x1, Pallas kernels, body(): pl.pallas_call(main_kernel, out_shape=(flat, flat, flat, full, full, full...  10.6 us
    ppermute x1, starting transfers between devices, body(): folded = lax.ppermute(fold, ('zonal', 'merid'), mirror)  4.83 us
    ppermute x1, starting transfers between devices, body(): east = lax.ppermute(to_west, 'zonal', down)  3.04 us
    pallas_call x1, Pallas kernels, body(): pl.pallas_call(pack_kernel, grid=(1,), out_shape=(pack_shape, pack_shape,...  2.56 us
    ppermute x1, waiting for transfers between devices, body(): folded = lax.ppermute(fold, ('zonal', 'merid'), mirror)  2.48 us
    pallas_call x1, Pallas kernels, body(): pl.pallas_call(lambda *refs: prepare_kernel(rows * zonal, cols * merid, *...  2.48 us
    unnamed x11, local copies, waits for them, and re-layouts  2.17 us
  transfers between devices with their start and end apart: 4, of which 2 were waited for; matrix products, arithmetic and copies ran while one was open for 0% of the time, Pallas kernels for 0%

profile of v1, /device:TPU:1, one launch (start us, length us, event | category | flops | bytes accessed | tf_op | source)
XLA Modules:
  0.0 47.2 jit_solution(17233640099909458623)
XLA Ops:
  0.6 0.0 copy-start.3
  0.6 0.7 %copy-done.3 = s32[4,2]{0,1:T(2,128)S(1)} copy-done((s32[4,2]{0,1:T(2,128)S(1)}, s32[4,2]{0,1:T(2,128)}, u32[]{:S(2)}) %copy-start.3) | copy-done | bytes 56
  1.3 0.7 %copy.16.refs_1_ = s32[4,2]{1,0:T(4,128)} copy(s32[4,2]{0,1:T(2,128)S(1)} %copy-done.3) | data formatting | bytes 64 | tf_op args[7]
  2.0 0.6 %pad_add_fusion.refs_0_.place = s32[4]{0:T(128)} fusion(s32[1]{0:T(128)} %bitcast.3, s32[1]{0:T(128)} %bitcast.2, s32[1]{0:T(128)} %bitcast.1, s32[1]{0:T(128)} %bitcast), kind=kLoop, calls=%fused_computation.2 | loop fusion | flops 12 | bytes 32 | tf_op jit(solution)/shard_map/stack | solution.py:330
  2.6 2.5 %prepare.1 = (f32[8,16,512]{2,1,0:T(8,128)}, f32[152,512]{1,0:T(8,128)}, f32[166,512]{1,0:T(8,128)}) custom-call(s32[4]{0:T(128)} %pad_add_fusion.refs_0_.place, s32[4,2]{1,0:T(4,128)} %copy.16.refs_1_, f32[4]{0:T(128)} %refs_2_.1, f32[16,512]{1,0:T(8,128)} %refs_3_.1, f32[16,512]{1,0:T(8,128)} %refs_4_.1, f32[16,512]{1,0:T(8,128)} %refs_5_.1, ...), custom_call_target="tpu_custom_call" | custom-call | tf_op jit(solution)/shard_map/prepare/pallas_call | solution.py:332
  5.1 2.1 %collective-permute-start.1 = (f32[166,512]{1,0:T(8,128)}, f32[166,512]{1,0:T(8,128)S(1)}, u32[]{:S(2)}, u32[]{:S(2)}) collective-permute-start(f32[166,512]{1,0:T(8,128)} %get-tuple-element.14), channel_id=1, source_target_pairs={{0,2},{2,4},{4,6},{6,8},{8,10},{10,12},{12,14},{14,0},{1,3},{3,5},... | collective-permute-start | bytes 1019912 | tf_op jit(solution)/shard_map/ppermute | solution.py:347
  7.1 3.0 %collective-permute-start = (f32[152,512]{1,0:T(8,128)}, f32[152,512]{1,0:T(8,128)S(1)}, u32[]{:S(2)}, u32[]{:S(2)}) collective-permute-start(f32[152,512]{1,0:T(8,128)} %get-tuple-element.13), channel_id=1, source_target_pairs={{2,0},{4,2},{6,4},{8,6},{10,8},{12,10},{14,12},{0,14},{3,1},{5,3},... | collective-permute-start | bytes 933896 | tf_op jit(solution)/shard_map/ppermute | solution.py:346
  10.2 12.5 %collective-permute-done.east_a.east_b.east_in = f32[152,512]{1,0:T(8,128)S(1)} collective-permute-done((f32[152,512]{1,0:T(8,128)}, f32[152,512]{1,0:T(8,128)S(1)}, u32[]{:S(2)}, u32[]{:S(2)}) %collective-permute-start) | collective-permute-done | bytes 311328 | tf_op jit(solution)/shard_map/ppermute | solution.py:346
  22.7 0.0 copy-start.1
  22.7 0.0 collective-permute-done.1.west_a.west_b.west_in
  22.7 0.0 copy-start
  22.7 0.7 %copy-done.1 = f32[152,512]{1,0:T(8,128)} copy-done((f32[152,512]{1,0:T(8,128)}, f32[152,512]{1,0:T(8,128)S(1)}, u32[]{:S(2)}) %copy-start.1) | copy-done | bytes 311320
  23.4 0.1 copy-done
  23.5 2.6 %pack.1 = (f32[64,128]{1,0:T(8,128)}, f32[64,128]{1,0:T(8,128)}, f32[64,128]{1,0:T(8,128)}) custom-call(s32[4]{0:T(128)} %pad_add_fusion.refs_0_.place, f32[8,16,512]{2,1,0:T(8,128)} %get-tuple-element.12.fields_a.fields_b.fields, f32[14,16,512]{2,1,0:T(8,128)} %thick.1, f32[14,16,512]{2,1,0:T(8,128)} %vu.1, f32[14,16,512]{2,1,0:T(8,128)} %vv.1, ...), custom_call_target="tpu_custom_call" | custom-call | tf_op jit(solution)/shard_map/pack/pallas_call | solution.py:358
  26.1 0.8 %broadcast_select_fusion = f32[64,128]{1,0:T(8,128)S(1)} fusion(f32[64,128]{1,0:T(8,128)} %get-tuple-element.16, f32[64,128]{1,0:T(8,128)} %get-tuple-element.17, pred[]{:T(512)S(6)} %eq.9), kind=kLoop, calls=%fused_computation | loop fusion | flops 8192 | bytes 98305 | tf_op jit(solution)/shard_map/jit(_where)/select_n | solution.py:374
  26.9 1.8 %collective-permute-start.3 = (f32[64,128]{1,0:T(8,128)S(1)}, f32[64,128]{1,0:T(8,128)S(1)}, u32[]{:S(2)}, u32[]{:S(2)}) collective-permute-start(f32[64,128]{1,0:T(8,128)S(1)} %broadcast_select_fusion), channel_id=1, source_target_pairs={{0,1},{1,0},{2,3},{3,2},{4,5},{5,4},{6,7},{7,6},{8,9},{9,8},{10,11... | collective-permute-start | bytes 98312 | tf_op jit(solution)/shard_map/ppermute | solution.py:374
  28.7 0.0 copy-done.4
  28.7 4.8 %collective-permute-start.2 = (f32[64,128]{1,0:T(8,128)S(1)}, f32[64,128]{1,0:T(8,128)S(1)}, u32[]{:S(2)}, u32[]{:S(2)}) collective-permute-start(f32[64,128]{1,0:T(8,128)S(1)} %copy-done.4), channel_id=1, source_target_pairs={{1,15},{3,13},{5,11},{7,9},{9,7},{11,5},{13,3},{15,1},{17,31},{19,... | collective-permute-start | bytes 98312 | tf_op jit(solution)/shard_map/ppermute | solution.py:372
  33.5 0.0 collective-permute-done.3.south_in
  33.5 0.0 copy-start.2
  33.5 2.5 %collective-permute-done.2 = f32[64,128]{1,0:T(8,128)S(1)} collective-permute-done((f32[64,128]{1,0:T(8,128)S(1)}, f32[64,128]{1,0:T(8,128)S(1)}, u32[]{:S(2)}, u32[]{:S(2)}) %collective-permute-start.2) | collective-permute-done | bytes 32800 | tf_op jit(solution)/shard_map/ppermute | solution.py:372
  36.0 0.6 %broadcast_select_fusion.1.north_in = f32[64,128]{1,0:T(8,128)} fusion(f32[64,128]{1,0:T(8,128)S(1)} %collective-permute-done.2, f32[64,128]{1,0:T(8,128)S(1)} %collective-permute-done.3.south_in, pred[]{:T(512)S(6)} %eq.8), kind=kLoop, calls=%fused_computation.1 | loop fusion | flops 8192 | bytes 98305 | tf_op jit(solution)/shard_map/jit(_where)/select_n | solution.py:380
  36.6 0.0 copy-done.2
  36.6 10.6 %advance.1 = (f32[16,512]{1,0:T(8,128)}, f32[16,512]{1,0:T(8,128)}, f32[16,512]{1,0:T(8,128)}, f32[14,16,512]{2,1,0:T(8,128)}, f32[14,16,512]{2,1,0:T(8,128)}, /*index=5*/f32[14,16,512]{2,1,0:T(8,128)}) custom-call(s32[4]{0:T(128)} %pad_add_fusion.refs_0_.place, f32[8,16,512]{2,1,0:T(8,128)} %get-tuple-element.12.fields_a.fields_b.fields, ...), custom_call_target="tpu_custom_call" | custom-call | tf_op jit(solution)/shard_map/advance/pallas_call | solution.py:384
  (1 shorter events, 0.0 us)
Async XLA Ops:
  0.6 0.7 %copy-start.3 = (s32[4,2]{0,1:T(2,128)S(1)}, s32[4,2]{0,1:T(2,128)}, u32[]{:S(2)}) copy-start(s32[4,2]{0,1:T(2,128)} %param.17) | copy-start | bytes 100
  5.1 17.6 %collective-permute-start.1 = (f32[166,512]{1,0:T(8,128)}, f32[166,512]{1,0:T(8,128)S(1)}, u32[]{:S(2)}, u32[]{:S(2)}) collective-permute-start(f32[166,512]{1,0:T(8,128)} %get-tuple-element.14), channel_id=1, source_target_pairs={{0,2},{2,4},{4,6},{6,8},{8,10},{10,12},{12,14},{14,0},{1,3},{3,5},... | collective-permute-start | bytes 1019912 | tf_op jit(solution)/shard_map/ppermute | solution.py:347
  7.1 15.5 %collective-permute-start = (f32[152,512]{1,0:T(8,128)}, f32[152,512]{1,0:T(8,128)S(1)}, u32[]{:S(2)}, u32[]{:S(2)}) collective-permute-start(f32[152,512]{1,0:T(8,128)} %get-tuple-element.13), channel_id=1, source_target_pairs={{2,0},{4,2},{6,4},{8,6},{10,8},{12,10},{14,12},{0,14},{3,1},{5,3},... | collective-permute-start | bytes 933896 | tf_op jit(solution)/shard_map/ppermute | solution.py:346
  22.7 0.7 %copy-start.1 = (f32[152,512]{1,0:T(8,128)}, f32[152,512]{1,0:T(8,128)S(1)}, u32[]{:S(2)}) copy-start(f32[152,512]{1,0:T(8,128)S(1)} %collective-permute-done.east_a.east_b.east_in) | copy-start | bytes 933892
  22.7 0.8 %copy-start = (f32[166,512]{1,0:T(8,128)}, f32[166,512]{1,0:T(8,128)S(1)}, u32[]{:S(2)}) copy-start(f32[166,512]{1,0:T(8,128)S(1)} %collective-permute-done.1.west_a.west_b.west_in) | copy-start | bytes 1019908
  26.1 2.6 %copy-start.4 = (f32[64,128]{1,0:T(8,128)S(1)}, f32[64,128]{1,0:T(8,128)}, u32[]{:S(2)}) copy-start(f32[64,128]{1,0:T(8,128)} %get-tuple-element.15) | copy-start | bytes 98308
  26.9 6.7 %collective-permute-start.3 = (f32[64,128]{1,0:T(8,128)S(1)}, f32[64,128]{1,0:T(8,128)S(1)}, u32[]{:S(2)}, u32[]{:S(2)}) collective-permute-start(f32[64,128]{1,0:T(8,128)S(1)} %broadcast_select_fusion), channel_id=1, source_target_pairs={{0,1},{1,0},{2,3},{3,2},{4,5},{5,4},{6,7},{7,6},{8,9},{9,8},{10,11... | collective-permute-start | bytes 98312 | tf_op jit(solution)/shard_map/ppermute | solution.py:374
  28.7 7.3 %collective-permute-start.2 = (f32[64,128]{1,0:T(8,128)S(1)}, f32[64,128]{1,0:T(8,128)S(1)}, u32[]{:S(2)}, u32[]{:S(2)}) collective-permute-start(f32[64,128]{1,0:T(8,128)S(1)} %copy-done.4), channel_id=1, source_target_pairs={{1,15},{3,13},{5,11},{7,9},{9,7},{11,5},{13,3},{15,1},{17,31},{19,... | collective-permute-start | bytes 98312 | tf_op jit(solution)/shard_map/ppermute | solution.py:372
  33.5 3.1 %copy-start.2 = (f32[64,128]{1,0:T(8,128)}, f32[64,128]{1,0:T(8,128)S(1)}, u32[]{:S(2)}) copy-start(f32[64,128]{1,0:T(8,128)S(1)} %collective-permute-done.3.south_in) | copy-start | bytes 98308

commit v2 on v1

v2 whole, which is shorter than its diff:
```python
import math

import jax
import jax.numpy as jnp
from jax import lax
from jax.experimental import pallas as pl
from jax.experimental.pallas import tpu as pltpu
from jax.sharding import PartitionSpec as P


NSUB = 6
STEPS = 2
WAVE_LIMIT = 0.225
STRESS_SCALE = 0.1
FLUX_STEP = 0.05
PRESS_COEF = 0.05

FIELDS = 8
HALO = NSUB * STEPS
SLOT = 16
LANES = 128
EDGE = 8

VMEM = pl.BlockSpec(memory_space=pltpu.VMEM)
SMEM = pl.BlockSpec(memory_space=pltpu.SMEM)


def whole_mod(product, total):
    rest = product - jnp.floor(product * (1.0 / total)) * total
    rest = jnp.where(rest < 0.0, rest + total, rest)
    return jnp.where(rest >= total, rest - total, rest)


def prepare_kernel(
    total_x, total_y, seeds, scale, eta, bu, bv, thick, vu, vv, faces, base,
    fields, to_west, to_east, packs, strips_west, strips_east,
):
    layers, rows, cols = thick.shape
    modes = scale.shape[0]
    f32 = jnp.float32

    lane = lax.broadcasted_iota(jnp.int32, (rows, LANES), 1)
    sub = lax.broadcasted_iota(jnp.int32, (8, cols), 0)
    wave_x = jnp.zeros((rows, LANES), f32)
    wave_y = jnp.zeros((8, cols), f32)
    for m in range(modes):
        wave_x = jnp.where(lane == m, seeds[0, m].astype(f32), wave_x)
        wave_y = jnp.where(sub == m, seeds[1, m].astype(f32), wave_y)
    col = (lax.broadcasted_iota(jnp.int32, (rows, LANES), 0) + lax.axis_index("zonal") * rows).astype(f32)
    row = (lax.broadcasted_iota(jnp.int32, (8, cols), 1) + lax.axis_index("merid") * cols).astype(f32)
    angle_x = whole_mod(wave_x * col, total_x) * (2.0 * math.pi / total_x)
    angle_y = whole_mod(wave_y * row, total_y) * (2.0 * math.pi / total_y)
    cos_x, sin_x = jnp.cos(angle_x), jnp.sin(angle_x)
    cos_y, sin_y = jnp.cos(angle_y), jnp.sin(angle_y)
    sum_cos = base[0]
    sum_sin = base[1]
    for m in range(modes):
        amp = scale[m]
        ca = cos_x[:, m : m + 1] * amp
        sa = sin_x[:, m : m + 1] * amp
        cb = cos_y[m : m + 1, :]
        sb = sin_y[m : m + 1, :]
        sum_cos = sum_cos + (ca * cb - sa * sb)
        sum_sin = sum_sin + (sa * cb + ca * sb)
    fields[0] = eta[...]
    fields[1] = bu[...]
    fields[2] = bv[...]
    total = thick[0]
    for k in range(1, layers):
        total = total + thick[k]
    fields[3] = total
    fields[4] = faces[0].astype(f32)
    fields[5] = faces[1].astype(f32)
    fields[6] = STRESS_SCALE * sum_cos
    fields[7] = STRESS_SCALE * sum_sin
    for f in range(FIELDS):
        value = fields[f]
        to_west[f * HALO : (f + 1) * HALO, :] = value[:HALO]
        to_east[f * HALO : (f + 1) * HALO, :] = value[rows - HALO :]
    for side, low in enumerate((True, False)):
        tile = slice(0, LANES) if low else slice(cols - LANES, cols)
        acc = jnp.zeros((rows, LANES), f32)
        for f in range(FIELDS):
            moved = pltpu.roll(fields[f, :, tile], (f * SLOT + (0 if low else SLOT)) % LANES, 1)
            acc = jnp.where(lane // SLOT == f, moved, acc)
        deep = jnp.zeros((rows, LANES), f32)
        for s, own in enumerate((thick, vu, vv)):
            for k in range(layers):
                at = 2 * (s * layers + k)
                moved = pltpu.roll(own[k, :, tile], (at + (0 if low else 2)) % LANES, 1)
                deep = jnp.where(lane // 2 == s * layers + k, moved, deep)
        packs[2 * side] = acc
        packs[2 * side + 1] = deep
    for side in range(2):
        acc = packs[2 * side]
        strips_west[side * HALO : (side + 1) * HALO, :] = acc[:HALO]
        strips_east[side * HALO : (side + 1) * HALO, :] = acc[rows - HALO :]
        deep = packs[2 * side + 1]
        strips_west[2 * HALO + side : 2 * HALO + side + 1, :] = deep[:1]
        strips_east[2 * HALO + side : 2 * HALO + side + 1, :] = deep[rows - 1 :]
    used = 2 * HALO + 2
    strips_west[used:, :] = jnp.zeros((strips_west.shape[0] - used, LANES), f32)
    strips_east[used:, :] = jnp.zeros((strips_east.shape[0] - used, LANES), f32)


def edges_kernel(thick, vu, vv, after, to_west, to_east):
    layers, rows, _ = thick.shape
    n = layers
    for k in range(layers):
        to_west[k : k + 1, :] = thick[k, 0:1, :]
        to_west[n + k : n + k + 1, :] = vu[k, 0:1, :] * ((thick[k, 0:1, :] + thick[k, 1:2, :]) * 0.5)
        to_west[2 * n + k : 2 * n + k + 1, :] = vv[k, 0:1, :]
        near = thick[k, rows - 2 : rows - 1, :]
        last = thick[k, rows - 1 : rows, :]
        to_east[k : k + 1, :] = last
        to_east[n + k : n + k + 1, :] = vu[k, rows - 2 : rows - 1, :] * ((near + last) * 0.5)
        to_east[2 * n + k : 2 * n + k + 1, :] = vu[k, rows - 1 : rows, :]
        to_east[3 * n + k : 3 * n + k + 1, :] = vv[k, rows - 1 : rows, :]


def fill_fields(target, f, fields, east, west, rows):
    cols = fields.shape[-1]
    target[f, 0:rows, 0:cols] = fields[f]
    target[f, rows : rows + HALO, 0:cols] = east[f * HALO : (f + 1) * HALO, :]
    target[f, rows + HALO : rows + 2 * HALO, 0:cols] = west[f * HALO : (f + 1) * HALO, :]


def fill_layers(target, k, layers, thick, vu, vv, east, west, rows):
    cols = thick.shape[-1]
    n = layers
    e, w = rows, rows + EDGE
    zero = jnp.zeros((EDGE, cols), jnp.float32)
    for s, own in enumerate((thick, vu, vv)):
        target[s * n + k, 0:rows, 0:cols] = own[k]
        target[s * n + k, rows : rows + EDGE, 0:cols] = zero
    target[k, e : e + 1, 0:cols] = east[k : k + 1, :]
    target[k, w - 1 : w, 0:cols] = west[k : k + 1, :]
    target[n + k, e : e + 1, 0:cols] = east[n + k : n + k + 1, :]
    target[n + k, w - 2 : w - 1, 0:cols] = west[n + k : n + k + 1, :]
    target[n + k, w - 1 : w, 0:cols] = west[2 * n + k : 2 * n + k + 1, :]
    target[2 * n + k, e : e + 1, 0:cols] = east[2 * n + k : 2 * n + k + 1, :]
    target[2 * n + k, w - 1 : w, 0:cols] = west[3 * n + k : 3 * n + k + 1, :]


def flipped(pack, rows, group):
    size = pack.shape[0]
    q = lax.broadcasted_iota(jnp.int32, (size, size), 0)
    p = lax.broadcasted_iota(jnp.int32, (size, size), 1)
    source = rows - 1 - q
    source = jnp.where(source < 0, source + size, source)
    flip_rows = (p == source).astype(jnp.float32)
    a = lax.broadcasted_iota(jnp.int32, (LANES, LANES), 0)
    b = lax.broadcasted_iota(jnp.int32, (LANES, LANES), 1)
    inner = jnp.bitwise_and(b, group - 1)
    flip_lanes = (a == b - inner + (group - 1 - inner)).astype(jnp.float32)
    half = jnp.dot(flip_rows, pack, precision=lax.Precision.HIGHEST, preferred_element_type=jnp.float32)
    return jnp.dot(half, flip_lanes, precision=lax.Precision.HIGHEST, preferred_element_type=jnp.float32)


def pack_kernel(merid, packs, east, west, swap, high, fold):
    rows = packs.shape[1]
    tall = rows + 2 * HALO
    short = rows + EDGE
    at_bottom = lax.axis_index("merid") == 0
    both = []
    for side in range(2):
        acc = jnp.concatenate(
            [packs[2 * side], east[side * HALO : (side + 1) * HALO, :], west[side * HALO : (side + 1) * HALO, :]], axis=0
        )
        high[tall : tall + rows, :] = packs[2 * side + 1]
        high[tall + rows :, :] = jnp.zeros((EDGE, LANES), jnp.float32)
        row = 2 * HALO + side
        high[tall + rows : tall + rows + 1, :] = east[row : row + 1, :]
        high[tall + short - 1 : tall + short, :] = west[row : row + 1, :]
        both.append((acc, high[tall : tall + short, :]))
    (low_f, low_l), (high_f, high_l) = both
    high[0:tall, :] = high_f
    if merid == 2:
        low_f = jnp.where(at_bottom, high_f, low_f)
        low_l = jnp.where(at_bottom, high_l, low_l)
    swap[0:tall, :] = low_f
    swap[tall : tall + short, :] = low_l
    fold[0:tall, :] = flipped(high_f, rows, SLOT)
    fold[tall : tall + short, :] = flipped(high_l, rows, 2)


def make_neighbours(ghost, cols):
    def east(a):
        n = a.shape[0]
        g = ghost[n]
        plus = pltpu.roll(a, n - 1, 0)
        return jnp.concatenate(
            [plus[:, :cols], jnp.where(g, pltpu.roll(a[:, cols:], 1, 0), plus[:, cols:])], axis=1
        )

    def west(a):
        n = a.shape[0]
        g = ghost[n]
        minus = pltpu.roll(a, 1, 0)
        return jnp.concatenate(
            [minus[:, :cols], jnp.where(g, pltpu.roll(a[:, cols:], n - 1, 0), minus[:, cols:])], axis=1
        )

    def north(a):
        g = ghost[a.shape[0]]
        plus = pltpu.roll(a, cols + LANES - 1, 1)
        minus = pltpu.roll(a[:, cols - LANES :], 1, 1)[:, LANES:]
        return jnp.concatenate([plus[:, :cols], jnp.where(g, minus, plus[:, cols:])], axis=1)

    def south(a):
        g = ghost[a.shape[0]]
        minus = pltpu.roll(a, 1, 1)
        plus = pltpu.roll(a[:, cols:], LANES - 1, 1)
        return jnp.concatenate([minus[:, :cols], jnp.where(g, plus, minus[:, cols:])], axis=1)

    return east, west, north, south


def setting(merid, sizes, cols):
    m = lax.axis_index("merid")
    top = m == merid - 1
    lanes = {n: lax.broadcasted_iota(jnp.int32, (n, LANES), 1) for n in sizes}
    ghost = {n: jnp.logical_and(top, lanes[n] < LANES // 2) for n in sizes}
    return m == 0, top, lanes, make_neighbours(ghost, cols)


def wide_kernel(
    merid, layers, fields, east_in, west_in, north_in, south_in, fold_in, out_eta, out_bu, out_bv, shared, wide,
):
    _, rows, cols = fields.shape
    tall = rows + 2 * HALO
    short = rows + EDGE
    bottom, top, lanes, (east, west, north, south) = setting(merid, (tall, short), cols)

    pack_n = jnp.where(top, fold_in[0:tall, :], north_in[0:tall, :])
    pack_s = jnp.where(bottom, 0.0, south_in[0:tall, :])
    for f in range(FIELDS):
        fill_fields(wide, f, fields, east_in, west_in, rows)
        up = pltpu.roll(pack_n, (-f * SLOT) % LANES, 1)
        down = pltpu.roll(pack_s, (LANES - SLOT - f * SLOT) % LANES, 1)
        edge = jnp.where(lanes[tall] >= LANES - SLOT, down, 0.0)
        wide[f, :, cols:] = jnp.where(lanes[tall] < SLOT, up, edge)

    near = lax.broadcasted_iota(jnp.int32, (EDGE, cols + LANES), 0) < EDGE // 2

    def shorten(a):
        return jnp.concatenate([a[:rows], jnp.where(near, a[rows : rows + EDGE], a[tall - EDGE :])], axis=0)

    total = wide[3]
    total_short = shorten(total)
    depth_u = (total_short + east(total_short)) * 0.5
    depth_v = (total_short + north(total_short)) * 0.5
    shared[0] = 1.0 / jnp.where(depth_u > 0.0, depth_u, 1.0)
    shared[1] = 1.0 / jnp.where(depth_v > 0.0, depth_v, 1.0)
    shared[2] = shorten(wide[4])
    shared[3] = shorten(wide[5])
    wide[3] = (WAVE_LIMIT / layers) * total
    eta = wide[0]
    bu = wide[1]
    bv = wide[2]
    for step in range(STEPS):
        sum_u = jnp.zeros_like(bu)
        sum_v = jnp.zeros_like(bv)
        for _ in range(NSUB):
            eta = eta - (bu - west(bu) + bv - south(bv))
            bu = wide[4] * (bu - wide[3] * (east(eta) - eta) + wide[6])
            bv = wide[5] * (bv - wide[3] * (north(eta) - eta) + wide[7])
            sum_u = sum_u + bu
            sum_v = sum_v + bv
        shared[4 + 2 * step] = shorten(sum_u) * (1.0 / NSUB)
        shared[5 + 2 * step] = shorten(sum_v) * (1.0 / NSUB)
    out_eta[...] = eta[:rows, :cols]
    out_bu[...] = bu[:rows, :cols]
    out_bv[...] = bv[:rows, :cols]


def layers_kernel(
    merid, thick, vu, vv, east_in, west_in, north_in, south_in, fold_in, shared, out_h, out_u, out_v, deep,
):
    layers, rows, cols = thick.shape
    tall = rows + 2 * HALO
    short = rows + EDGE
    bottom, top, lanes, (east, west, north, south) = setting(merid, (short,), cols)
    deep_n = jnp.where(top, fold_in[tall : tall + short, :], north_in[tall : tall + short, :])
    deep_s = jnp.where(bottom, 0.0, south_in[tall : tall + short, :])
    for k in range(layers):
        fill_layers(deep, k, layers, thick, vu, vv, east_in, west_in, rows)
    for k in range(3 * layers):
        up = pltpu.roll(deep_n, (-2 * k) % LANES, 1)
        down = pltpu.roll(deep_s, (LANES - 2 - 2 * k) % LANES, 1)
        edge = jnp.where(lanes[short] >= LANES - 2, down, 0.0)
        deep[k, :, cols:] = jnp.where(lanes[short] < 2, up, edge)
    spot = lax.broadcasted_iota(jnp.int32, (short, cols), 0)
    given = jnp.logical_or(spot == rows, spot == short - 2)

    for step in range(STEPS):
        last = step == STEPS - 1

        def first_pass(k, carry):
            press_u, press_v, total_u, total_v = carry
            h = deep[k]
            u = deep[layers + k]
            v = deep[2 * layers + k]
            east_h = east(h)
            north_h = north(h)
            thick_u = (h + east_h) * 0.5
            thick_v = (h + north_h) * 0.5
            press_u = press_u + (east_h - h)
            press_v = press_v + (north_h - h)
            trial_u = u - PRESS_COEF * press_u
            trial_v = v - PRESS_COEF * press_v
            flux_u = u * thick_u
            if not last:
                flux_u = jnp.concatenate([jnp.where(given, u[:, :cols], flux_u[:, :cols]), flux_u[:, cols:]], axis=1)
            flux_v = v * thick_v
            new = h - FLUX_STEP * (flux_u - west(flux_u) + flux_v - south(flux_v))
            if last:
                out_h[k] = new[:rows, :cols]
            else:
                deep[k] = new
            deep[layers + k] = trial_u
            deep[2 * layers + k] = trial_v
            return press_u, press_v, total_u + thick_u * trial_u, total_v + thick_v * trial_v

        zero = jnp.zeros((short, cols + LANES), jnp.float32)
        _, _, total_u, total_v = lax.fori_loop(0, layers, first_pass, (zero, zero, zero, zero))
        fix_u = (shared[4 + 2 * step] - total_u) * shared[0]
        fix_v = (shared[5 + 2 * step] - total_v) * shared[1]

        def second_pass(k, carry):
            new_u = shared[2] * (deep[layers + k] + fix_u)
            new_v = shared[3] * (deep[2 * layers + k] + fix_v)
            if last:
                out_u[k] = new_u[:rows, :cols]
                out_v[k] = new_v[:rows, :cols]
            else:
                deep[layers + k] = new_u
                deep[2 * layers + k] = new_v
            return carry

        lax.fori_loop(0, layers, second_pass, 0)


def body(
    height,
    transport_u,
    transport_v,
    thickness,
    velocity_u,
    velocity_v,
    sea_faces,
    wind_seeds,
    wind_scale,
    wind_base,
):
    layers, rows, cols = thickness.shape
    f32 = jnp.float32
    zonal = lax.axis_size("zonal")
    merid = lax.axis_size("merid")
    tall = rows + 2 * HALO
    short = rows + EDGE

    def shape(*dims):
        return jax.ShapeDtypeStruct(dims, f32)

    fields, wide_west, wide_east, packs, strips_west, strips_east = pl.pallas_call(
        lambda *refs: prepare_kernel(rows * zonal, cols * merid, *refs),
        out_shape=(
            shape(FIELDS, rows, cols),
            shape(FIELDS * HALO, cols),
            shape(FIELDS * HALO, cols),
            shape(4, rows, LANES),
            shape(2 * HALO + EDGE, LANES),
            shape(2 * HALO + EDGE, LANES),
        ),
        in_specs=[SMEM, SMEM] + [VMEM] * 8,
        out_specs=(VMEM,) * 6,
        name="prepare",
    )(wind_seeds.T, wind_scale, height, transport_u, transport_v, thickness, velocity_u, velocity_v, sea_faces, wind_base)

    up = [(i, (i + 1) % zonal) for i in range(zonal)]
    down = [(j, i) for i, j in up]
    strips_from_east = lax.ppermute(strips_west, "zonal", down)
    strips_from_west = lax.ppermute(strips_east, "zonal", up)
    wide_from_east = lax.ppermute(wide_west, "zonal", down)
    wide_from_west = lax.ppermute(wide_east, "zonal", up)

    deep_west, deep_east = pl.pallas_call(
        edges_kernel,
        out_shape=(shape(3 * layers, cols), shape(4 * layers, cols)),
        in_specs=[VMEM] * 3 + [pl.BlockSpec(memory_space=pl.ANY)],
        out_specs=(VMEM, VMEM),
        name="edges",
    )(thickness, velocity_u, velocity_v, strips_west)
    deep_from_east = lax.ppermute(deep_west, "zonal", down)
    deep_from_west = lax.ppermute(deep_east, "zonal", up)

    swap, high, fold = pl.pallas_call(
        lambda *refs: pack_kernel(merid, *refs),
        out_shape=(shape(tall + short, LANES),) * 3,
        in_specs=[VMEM] * 3,
        out_specs=(VMEM,) * 3,
        name="pack",
    )(packs, strips_from_east, strips_from_west)

    mirror = [(i * merid + merid - 1, (zonal - 1 - i) * merid + merid - 1) for i in range(zonal)]
    folded = lax.ppermute(fold, ("zonal", "merid"), mirror)
    if merid == 2:
        from_north = lax.ppermute(swap, "merid", [(0, 1), (1, 0)])
        from_south = from_north
    else:
        from_north = lax.ppermute(swap, "merid", [(i + 1, i) for i in range(merid - 1)])
        from_south = lax.ppermute(high, "merid", [(i, i + 1) for i in range(merid - 1)])

    flat = shape(rows, cols)
    full = shape(layers, rows, cols)
    eta, bu, bv, shared = pl.pallas_call(
        lambda *refs: wide_kernel(merid, layers, *refs),
        out_shape=(flat, flat, flat, shape(4 + 2 * STEPS, short, cols + LANES)),
        in_specs=[VMEM] * 6,
        out_specs=(VMEM,) * 4,
        scratch_shapes=[pltpu.VMEM((FIELDS, tall, cols + LANES), f32)],
        name="barotropic",
    )(fields, wide_from_east, wide_from_west, from_north, from_south, folded)
    h, u, v = pl.pallas_call(
        lambda *refs: layers_kernel(merid, *refs),
        out_shape=(full, full, full),
        in_specs=[VMEM] * 9,
        out_specs=(VMEM,) * 3,
        scratch_shapes=[pltpu.VMEM((3 * layers, short, cols + LANES), f32)],
        name="layers",
    )(thickness, velocity_u, velocity_v, deep_from_east, deep_from_west, from_north, from_south, folded, shared)
    return eta, bu, bv, h, u, v


def solution(mesh):
    placed = (
        P(("members", "zonal"), "merid"),
        P(("members", "zonal"), "merid"),
        P(("members", "zonal"), "merid"),
        P(None, ("members", "zonal"), "merid"),
        P(None, ("members", "zonal"), "merid"),
        P(None, ("members", "zonal"), "merid"),
        P(None, "zonal", "merid"),
        P("members", None),
        P("members"),
        P(None, "zonal", "merid"),
    )

    return jax.shard_map(
        body,
        mesh=mesh,
        in_specs=placed,
        out_specs=(
            P(("members", "zonal"), "merid"),
            P(("members", "zonal"), "merid"),
            P(("members", "zonal"), "merid"),
            P(None, ("members", "zonal"), "merid"),
            P(None, ("members", "zonal"), "merid"),
            P(None, ("members", "zonal"), "merid"),
        ),
        check_vma=False,
    )
```

time: 47.5 us -> 53 us (1.12)
  starting transfers between devices: 11.7 us -> 21.9 us
  waiting for transfers between devices: 15 us -> 8.94 us
  Pallas kernels: 15.6 us -> 19.2 us
  other arithmetic: 2.01 us -> 0 us
    ppermute x3 -> x7, starting transfers between devices: 6.91 us -> 15.3 us  [the longest x1 5.11 us: body(): wide_from_east = lax.ppermute(wide_west, 'zonal', down)]
    ppermute x3 -> x7, waiting for transfers between devices: 12.5 us -> 7.44 us  [the longest x1 5.49 us: body(): strips_from_west = lax.ppermute(strips_east, 'zonal', up)]
    pallas_call x2 -> x4, Pallas kernels: 13.1 us -> 16.7 us  [the longest x1 8.61 us: body(): pl.pallas_call(lambda *refs: layers_kernel(merid, *refs), out_shape=(full...]
    ppermute x1, starting transfers between devices: 4.83 us -> 6.61 us  [body(): folded = lax.ppermute(fold, ('zonal', 'merid'), mirror)]
    select_n x2 -> x0, other arithmetic: 1.4 us -> none  [the longest x1 0.78 us: body(): jnp.where(m == 0, high, low)]
    ppermute x1, waiting for transfers between devices: 2.48 us -> 1.5 us  [body(): folded = lax.ppermute(fold, ('zonal', 'merid'), mirror)]
    another operation x1 -> x0, other arithmetic: 0.61 us -> none  [body(): jnp.stack([z, m, (m == merid - 1).astype(jnp.int32), (m == 0).astype(jnp....]
    unnamed x11 -> x20, local copies, waits for them, and re-layouts: 2.17 us -> 1.98 us
  transfers between devices with their start and end apart: 4 -> 8, of which waited for: 2 -> 4; matrix products, arithmetic and copies ran while one was open for 0% -> 0% of each run, Pallas kernels for 0% -> 15%
where the time goes in v2:
time: 53 us; the launch traced here: 52.7 us
  starting transfers between devices  21.9 us (41%)
  Pallas kernels  19.2 us (36%)
  waiting for transfers between devices  8.94 us (17%)
  local copies, waits for them, and re-layouts  1.98 us (4%)
  between operations  0.71 us (1%)
    pallas_call x1, Pallas kernels, body(): pl.pallas_call(lambda *refs: layers_kernel(merid, *refs), out_shape=(full...  8.61 us
    ppermute x1, starting transfers between devices, body(): folded = lax.ppermute(fold, ('zonal', 'merid'), mirror)  6.61 us
    ppermute x1, waiting for transfers between devices, body(): strips_from_west = lax.ppermute(strips_east, 'zonal', up)  5.49 us
    ppermute x1, starting transfers between devices, body(): wide_from_east = lax.ppermute(wide_west, 'zonal', down)  5.11 us
    pallas_call x1, Pallas kernels, body(): pl.pallas_call(lambda *refs: wide_kernel(merid, layers, *refs), out_shape...  4.22 us
    ppermute x1, starting transfers between devices, body(): deep_from_east = lax.ppermute(deep_west, 'zonal', down)  4.21 us
    ppermute x1, starting transfers between devices, body(): strips_from_east = lax.ppermute(strips_west, 'zonal', down)  3.25 us
    ppermute x1, starting transfers between devices, body(): from_north = lax.ppermute(swap, 'merid', [(0, 1), (1, 0)])  2.66 us
  transfers between devices with their start and end apart: 8, of which 4 were waited for; matrix products, arithmetic and copies ran while one was open for 0% of the time, Pallas kernels for 15%

profile of v2, /device:TPU:1, one launch (start us, length us, event | category | flops | bytes accessed | tf_op | source)
XLA Modules:
  0.0 52.7 jit_solution(14149227574530159270)
XLA Ops:
  0.6 2.5 %prepare.1 = (f32[8,16,512]{2,1,0:T(8,128)}, f32[96,512]{1,0:T(8,128)}, f32[96,512]{1,0:T(8,128)}, f32[4,16,128]{2,1,0:T(8,128)}, f32[32,128]{1,0:T(8,128)}, /*index=5*/f32[32,128]{1,0:T(8,128)}) custom-call(s32[2,4]{1,0:T(2,128)} %bitcast.1, f32[4]{0:T(128)} %refs_1_.2, f32[16,512]{1,0:T(8,128)} %refs_2_.2, f32[16,512]{1,0:T(8,128)} %refs_3_.1, ...), custom_call_target="tpu_custom_call" | custom-call | tf_op jit(solution)/shard_map/prepare/pallas_call | solution.py:366
  3.1 5.1 %collective-permute-start = (f32[96,512]{1,0:T(8,128)}, f32[96,512]{1,0:T(8,128)S(1)}, u32[]{:S(2)}, u32[]{:S(2)}) collective-permute-start(f32[96,512]{1,0:T(8,128)} %get-tuple-element.24), channel_id=1, source_target_pairs={{2,0},{4,2},{6,4},{8,6},{10,8},{12,10},{14,12},{0,14},{3,1},{5,3},... | collective-permute-start | bytes 589832 | tf_op jit(solution)/shard_map/ppermute | solution.py:385
  8.2 0.0 collective-permute-start.1
  8.2 2.1 %edges.1 = (f32[42,512]{1,0:T(8,128)}, f32[56,512]{1,0:T(8,128)}) custom-call(f32[14,16,512]{2,1,0:T(8,128)} %refs_0_.1, f32[14,16,512]{2,1,0:T(8,128)} %refs_1_.3, f32[14,16,512]{2,1,0:T(8,128)} %refs_2_.3, f32[32,128]{1,0:T(8,128)} %get-tuple-element.27.after), custom_call_target="tpu_custom_call" | custom-call | tf_op jit(solution)/shard_map/edges/pallas_call | solution.py:388
  10.3 0.0 collective-permute-start.7
  10.3 0.0 collective-permute-start.3
  10.4 4.2 %collective-permute-start.6 = (f32[42,512]{1,0:T(8,128)}, f32[42,512]{1,0:T(8,128)S(1)}, u32[]{:S(2)}, u32[]{:S(2)}) collective-permute-start(f32[42,512]{1,0:T(8,128)} %get-tuple-element.34), channel_id=1, source_target_pairs={{2,0},{4,2},{6,4},{8,6},{10,8},{12,10},{14,12},{0,14},{3,1},{5,3},... | collective-permute-start | bytes 258056 | tf_op jit(solution)/shard_map/ppermute | solution.py:395
  14.6 5.5 %collective-permute-done.3.refs_2_ = f32[32,128]{1,0:T(8,128)S(1)} collective-permute-done((f32[32,128]{1,0:T(8,128)S(1)}, f32[32,128]{1,0:T(8,128)S(1)}, u32[]{:S(2)}, u32[]{:S(2)}) %collective-permute-start.3) | collective-permute-done | bytes 16416 | tf_op jit(solution)/shard_map/ppermute | solution.py:384
  20.1 3.2 %collective-permute-start.2 = (f32[32,128]{1,0:T(8,128)S(1)}, f32[32,128]{1,0:T(8,128)S(1)}, u32[]{:S(2)}, u32[]{:S(2)}) collective-permute-start(f32[32,128]{1,0:T(8,128)S(1)} %copy-done.6), channel_id=1, source_target_pairs={{2,0},{4,2},{6,4},{8,6},{10,8},{12,10},{14,12},{0,14},{3,1},{5,3},... | collective-permute-start | bytes 49160 | tf_op jit(solution)/shard_map/ppermute | solution.py:383
  23.3 0.9 %collective-permute-done.2.refs_1_ = f32[32,128]{1,0:T(8,128)S(1)} collective-permute-done((f32[32,128]{1,0:T(8,128)S(1)}, f32[32,128]{1,0:T(8,128)S(1)}, u32[]{:S(2)}, u32[]{:S(2)}) %collective-permute-start.2) | collective-permute-done | bytes 16416 | tf_op jit(solution)/shard_map/ppermute | solution.py:383
  24.2 0.6 %copy-done.8 = f32[32,128]{1,0:T(8,128)} copy-done((f32[32,128]{1,0:T(8,128)}, f32[32,128]{1,0:T(8,128)S(1)}, u32[]{:S(2)}) %copy-start.8) | copy-done | bytes 16408
  24.8 1.8 %pack.1 = (f32[64,128]{1,0:T(8,128)}, f32[64,128]{1,0:T(8,128)}, f32[64,128]{1,0:T(8,128)}) custom-call(f32[4,16,128]{2,1,0:T(8,128)} %get-tuple-element.26.refs_0_, f32[32,128]{1,0:T(8,128)} %copy-done.8, f32[32,128]{1,0:T(8,128)} %copy-done.7), custom_call_target="tpu_custom_call" | custom-call | tf_op jit(solution)/shard_map/pack/pallas_call | solution.py:398
  26.6 2.7 %collective-permute-start.4 = (f32[64,128]{1,0:T(8,128)}, f32[64,128]{1,0:T(8,128)S(1)}, u32[]{:S(2)}, u32[]{:S(2)}) collective-permute-start(f32[64,128]{1,0:T(8,128)} %get-tuple-element.29), channel_id=1, source_target_pairs={{0,1},{1,0},{2,3},{3,2},{4,5},{5,4},{6,7},{7,6},{8,9},{9,8},{10,11... | collective-permute-start | bytes 98312 | tf_op jit(solution)/shard_map/ppermute | solution.py:409
  29.3 1.1 %collective-permute-done.4.refs_3_.refs_4_.refs_5_.refs_6_ = f32[64,128]{1,0:T(8,128)S(1)} collective-permute-done((f32[64,128]{1,0:T(8,128)}, f32[64,128]{1,0:T(8,128)S(1)}, u32[]{:S(2)}, u32[]{:S(2)}) %collective-permute-start.4) | collective-permute-done | bytes 32800 | tf_op jit(solution)/shard_map/ppermute | solution.py:409
  30.4 6.6 %collective-permute-start.5 = (f32[64,128]{1,0:T(8,128)}, f32[64,128]{1,0:T(8,128)S(1)}, u32[]{:S(2)}, u32[]{:S(2)}) collective-permute-start(f32[64,128]{1,0:T(8,128)} %get-tuple-element.30), channel_id=1, source_target_pairs={{1,15},{3,13},{5,11},{7,9},{9,7},{11,5},{13,3},{15,1},{17,31},{19,... | collective-permute-start | bytes 98312 | tf_op jit(solution)/shard_map/ppermute | solution.py:407
  37.0 1.5 %collective-permute-done.5.refs_5_.refs_7_ = f32[64,128]{1,0:T(8,128)S(1)} collective-permute-done((f32[64,128]{1,0:T(8,128)}, f32[64,128]{1,0:T(8,128)S(1)}, u32[]{:S(2)}, u32[]{:S(2)}) %collective-permute-start.5) | collective-permute-done | bytes 32800 | tf_op jit(solution)/shard_map/ppermute | solution.py:407
  38.5 0.0 copy-start.2
  38.5 0.6 %copy-done.3 = f32[64,128]{1,0:T(8,128)} copy-done((f32[64,128]{1,0:T(8,128)}, f32[64,128]{1,0:T(8,128)S(1)}, u32[]{:S(2)}) %copy-start.3) | copy-done | bytes 32792
  39.1 0.1 copy-done.1
  39.2 0.1 copy-done.2
  39.2 4.2 %barotropic.1 = (f32[16,512]{1,0:T(8,128)}, f32[16,512]{1,0:T(8,128)}, f32[16,512]{1,0:T(8,128)}, f32[8,24,640]{2,1,0:T(8,128)}) custom-call(f32[8,16,512]{2,1,0:T(8,128)} %get-tuple-element.23.refs_0_, f32[96,512]{1,0:T(8,128)} %copy-done.1, f32[96,512]{1,0:T(8,128)} %copy-done.2, f32[64,128]{1,0:T(8,128)} %copy-done, f32[64,128]{1,0:T(8,128)} %copy-done, ...), custom_call_target="tpu_custom_call" | custom-call | tf_op jit(solution)/shard_map/barotropic/pallas_call | solution.py:417
  43.5 0.6 %copy-done.5 = f32[42,512]{1,0:T(8,128)} copy-done((f32[42,512]{1,0:T(8,128)}, f32[42,512]{1,0:T(8,128)S(1)}, u32[]{:S(2)}) %copy-start.5) | copy-done | bytes 86040
  44.1 0.0 copy-done.4
  44.1 8.6 %layers.1 = (f32[14,16,512]{2,1,0:T(8,128)}, f32[14,16,512]{2,1,0:T(8,128)}, f32[14,16,512]{2,1,0:T(8,128)}) custom-call(f32[14,16,512]{2,1,0:T(8,128)} %refs_0_.1, f32[14,16,512]{2,1,0:T(8,128)} %refs_1_.3, f32[14,16,512]{2,1,0:T(8,128)} %refs_2_.3, f32[42,512]{1,0:T(8,128)} %copy-done.5, f32[56,512]{1,0:T(8,128)} %copy-done.4, f32[64,128]{1,0:T(8,128)} %copy-done, ...), custom_call_target="tpu_custom_call" | custom-call | tf_op jit(solution)/shard_map/layers/pallas_call | solution.py:425
  (17 shorter events, 0.0 us)
Async XLA Ops:
  3.1 35.3 %collective-permute-start = (f32[96,512]{1,0:T(8,128)}, f32[96,512]{1,0:T(8,128)S(1)}, u32[]{:S(2)}, u32[]{:S(2)}) collective-permute-start(f32[96,512]{1,0:T(8,128)} %get-tuple-element.24), channel_id=1, source_target_pairs={{2,0},{4,2},{6,4},{8,6},{10,8},{12,10},{14,12},{0,14},{3,1},{5,3},... | collective-permute-start | bytes 589832 | tf_op jit(solution)/shard_map/ppermute | solution.py:385
  8.2 30.2 %collective-permute-start.1 = (f32[96,512]{1,0:T(8,128)}, f32[96,512]{1,0:T(8,128)S(1)}, u32[]{:S(2)}, u32[]{:S(2)}) collective-permute-start(f32[96,512]{1,0:T(8,128)} %get-tuple-element.25), channel_id=1, source_target_pairs={{0,2},{2,4},{4,6},{6,8},{8,10},{10,12},{12,14},{14,0},{1,3},{3,5},... | collective-permute-start | bytes 589832 | tf_op jit(solution)/shard_map/ppermute | solution.py:386
  8.2 2.1 %copy-start.9 = (f32[32,128]{1,0:T(8,128)S(1)}, f32[32,128]{1,0:T(8,128)}, u32[]{:S(2)}) copy-start(f32[32,128]{1,0:T(8,128)} %get-tuple-element.28) | copy-start | bytes 49156
  8.2 11.8 %copy-start.6 = (f32[32,128]{1,0:T(8,128)S(1)}, f32[32,128]{1,0:T(8,128)}, u32[]{:S(2)}) copy-start(f32[32,128]{1,0:T(8,128)} %get-tuple-element.27.after) | copy-start | bytes 49156
  10.3 33.2 %collective-permute-start.7 = (f32[56,512]{1,0:T(8,128)}, f32[56,512]{1,0:T(8,128)S(1)}, u32[]{:S(2)}, u32[]{:S(2)}) collective-permute-start(f32[56,512]{1,0:T(8,128)} %get-tuple-element.35), channel_id=1, source_target_pairs={{0,2},{2,4},{4,6},{6,8},{8,10},{10,12},{12,14},{14,0},{1,3},{3,5},... | collective-permute-start | bytes 344072 | tf_op jit(solution)/shard_map/ppermute | solution.py:396
  10.3 9.8 %collective-permute-start.3 = (f32[32,128]{1,0:T(8,128)S(1)}, f32[32,128]{1,0:T(8,128)S(1)}, u32[]{:S(2)}, u32[]{:S(2)}) collective-permute-start(f32[32,128]{1,0:T(8,128)S(1)} %copy-done.9), channel_id=1, source_target_pairs={{0,2},{2,4},{4,6},{6,8},{8,10},{10,12},{12,14},{14,0},{1,3},{3,5},... | collective-permute-start | bytes 49160 | tf_op jit(solution)/shard_map/ppermute | solution.py:384
  10.4 33.1 %collective-permute-start.6 = (f32[42,512]{1,0:T(8,128)}, f32[42,512]{1,0:T(8,128)S(1)}, u32[]{:S(2)}, u32[]{:S(2)}) collective-permute-start(f32[42,512]{1,0:T(8,128)} %get-tuple-element.34), channel_id=1, source_target_pairs={{2,0},{4,2},{6,4},{8,6},{10,8},{12,10},{14,12},{0,14},{3,1},{5,3},... | collective-permute-start | bytes 258056 | tf_op jit(solution)/shard_map/ppermute | solution.py:395
  20.1 4.1 %copy-start.7 = (f32[32,128]{1,0:T(8,128)}, f32[32,128]{1,0:T(8,128)S(1)}, u32[]{:S(2)}) copy-start(f32[32,128]{1,0:T(8,128)S(1)} %collective-permute-done.3.refs_2_) | copy-start | bytes 49156
  20.1 4.1 %collective-permute-start.2 = (f32[32,128]{1,0:T(8,128)S(1)}, f32[32,128]{1,0:T(8,128)S(1)}, u32[]{:S(2)}, u32[]{:S(2)}) collective-permute-start(f32[32,128]{1,0:T(8,128)S(1)} %copy-done.6), channel_id=1, source_target_pairs={{2,0},{4,2},{6,4},{8,6},{10,8},{12,10},{14,12},{0,14},{3,1},{5,3},... | collective-permute-start | bytes 49160 | tf_op jit(solution)/shard_map/ppermute | solution.py:383
  24.2 0.6 %copy-start.8 = (f32[32,128]{1,0:T(8,128)}, f32[32,128]{1,0:T(8,128)S(1)}, u32[]{:S(2)}) copy-start(f32[32,128]{1,0:T(8,128)S(1)} %collective-permute-done.2.refs_1_) | copy-start | bytes 49156
  26.6 3.7 %collective-permute-start.4 = (f32[64,128]{1,0:T(8,128)}, f32[64,128]{1,0:T(8,128)S(1)}, u32[]{:S(2)}, u32[]{:S(2)}) collective-permute-start(f32[64,128]{1,0:T(8,128)} %get-tuple-element.29), channel_id=1, source_target_pairs={{0,1},{1,0},{2,3},{3,2},{4,5},{5,4},{6,7},{7,6},{8,9},{9,8},{10,11... | collective-permute-start | bytes 98312 | tf_op jit(solution)/shard_map/ppermute | solution.py:409
  30.4 8.1 %copy-start = (f32[64,128]{1,0:T(8,128)}, f32[64,128]{1,0:T(8,128)S(1)}, u32[]{:S(2)}) copy-start(f32[64,128]{1,0:T(8,128)S(1)} %collective-permute-done.4.refs_3_.refs_4_.refs_5_.refs_6_) | copy-start | bytes 98308
  30.4 8.1 %collective-permute-start.5 = (f32[64,128]{1,0:T(8,128)}, f32[64,128]{1,0:T(8,128)S(1)}, u32[]{:S(2)}, u32[]{:S(2)}) collective-permute-start(f32[64,128]{1,0:T(8,128)} %get-tuple-element.30), channel_id=1, source_target_pairs={{1,15},{3,13},{5,11},{7,9},{9,7},{11,5},{13,3},{15,1},{17,31},{19,... | collective-permute-start | bytes 98312 | tf_op jit(solution)/shard_map/ppermute | solution.py:407
  38.5 0.6 %copy-start.3 = (f32[64,128]{1,0:T(8,128)}, f32[64,128]{1,0:T(8,128)S(1)}, u32[]{:S(2)}) copy-start(f32[64,128]{1,0:T(8,128)S(1)} %collective-permute-done.5.refs_5_.refs_7_) | copy-start | bytes 98308
  38.5 0.7 %copy-start.1 = (f32[96,512]{1,0:T(8,128)}, f32[96,512]{1,0:T(8,128)S(1)}, u32[]{:S(2)}) copy-start(f32[96,512]{1,0:T(8,128)S(1)} %collective-permute-done.refs_1_) | copy-start | bytes 589828
  38.5 0.7 %copy-start.2 = (f32[96,512]{1,0:T(8,128)}, f32[96,512]{1,0:T(8,128)S(1)}, u32[]{:S(2)}) copy-start(f32[96,512]{1,0:T(8,128)S(1)} %collective-permute-done.1.refs_2_) | copy-start | bytes 589828
  43.4 0.6 %copy-start.5 = (f32[42,512]{1,0:T(8,128)}, f32[42,512]{1,0:T(8,128)S(1)}, u32[]{:S(2)}) copy-start(f32[42,512]{1,0:T(8,128)S(1)} %collective-permute-done.6.refs_3_) | copy-start | bytes 258052
  43.5 0.7 %copy-start.4 = (f32[56,512]{1,0:T(8,128)}, f32[56,512]{1,0:T(8,128)S(1)}, u32[]{:S(2)}) copy-start(f32[56,512]{1,0:T(8,128)S(1)} %collective-permute-done.7.refs_4_) | copy-start | bytes 344068

commit v3 on v2

--- a/solution.py
+++ b/solution.py
@@ -77,6 +77,8 @@
         value = fields[f]
         to_west[f * HALO : (f + 1) * HALO, :] = value[:HALO]
         to_east[f * HALO : (f + 1) * HALO, :] = value[rows - HALO :]
+    start = FIELDS * HALO
+    edge_rows(thick, vu, vv, to_west.at[pl.ds(start, 3 * layers)], to_east.at[pl.ds(start, 4 * layers)])
     for side, low in enumerate((True, False)):
         tile = slice(0, LANES) if low else slice(cols - LANES, cols)
         acc = jnp.zeros((rows, LANES), f32)
@@ -103,7 +105,7 @@
     strips_east[used:, :] = jnp.zeros((strips_east.shape[0] - used, LANES), f32)
 
 
-def edges_kernel(thick, vu, vv, after, to_west, to_east):
+def edge_rows(thick, vu, vv, to_west, to_east):
     layers, rows, _ = thick.shape
     n = layers
     for k in range(layers):
@@ -341,6 +343,21 @@
         lax.fori_loop(0, layers, second_pass, 0)
 
 
+def advance_kernel(
+    merid, fields, thick, vu, vv, east_in, west_in, north_in, south_in, fold_in,
+    out_eta, out_bu, out_bv, out_h, out_u, out_v, shared, wide, deep,
+):
+    layers = thick.shape[0]
+    start = FIELDS * HALO
+    wide_kernel(
+        merid, layers, fields, east_in, west_in, north_in, south_in, fold_in, out_eta, out_bu, out_bv, shared, wide
+    )
+    layers_kernel(
+        merid, thick, vu, vv, east_in.at[pl.ds(start, 3 * layers)], west_in.at[pl.ds(start, 4 * layers)],
+        north_in, south_in, fold_in, shared, out_h, out_u, out_v, deep,
+    )
+
+
 def body(
     height,
     transport_u,
@@ -367,8 +384,8 @@
         lambda *refs: prepare_kernel(rows * zonal, cols * merid, *refs),
         out_shape=(
             shape(FIELDS, rows, cols),
-            shape(FIELDS * HALO, cols),
-            shape(FIELDS * HALO, cols),
+            shape(FIELDS * HALO + 3 * layers, cols),
+            shape(FIELDS * HALO + 4 * layers, cols),
             shape(4, rows, LANES),
             shape(2 * HALO + EDGE, LANES),
             shape(2 * HALO + EDGE, LANES),
@@ -385,16 +402,6 @@
     wide_from_east = lax.ppermute(wide_west, "zonal", down)
     wide_from_west = lax.ppermute(wide_east, "zonal", up)
 
-    deep_west, deep_east = pl.pallas_call(
-        edges_kernel,
-        out_shape=(shape(3 * layers, cols), shape(4 * layers, cols)),
-        in_specs=[VMEM] * 3 + [pl.BlockSpec(memory_space=pl.ANY)],
-        out_specs=(VMEM, VMEM),
-        name="edges",
-    )(thickness, velocity_u, velocity_v, strips_west)
-    deep_from_east = lax.ppermute(deep_west, "zonal", down)
-    deep_from_west = lax.ppermute(deep_east, "zonal", up)
-
     swap, high, fold = pl.pallas_call(
         lambda *refs: pack_kernel(merid, *refs),
         out_shape=(shape(tall + short, LANES),) * 3,
@@ -414,23 +421,18 @@
 
     flat = shape(rows, cols)
     full = shape(layers, rows, cols)
-    eta, bu, bv, shared = pl.pallas_call(
-        lambda *refs: wide_kernel(merid, layers, *refs),
-        out_shape=(flat, flat, flat, shape(4 + 2 * STEPS, short, cols + LANES)),
-        in_specs=[VMEM] * 6,
-        out_specs=(VMEM,) * 4,
-        scratch_shapes=[pltpu.VMEM((FIELDS, tall, cols + LANES), f32)],
-        name="barotropic",
-    )(fields, wide_from_east, wide_from_west, from_north, from_south, folded)
-    h, u, v = pl.pallas_call(
-        lambda *refs: layers_kernel(merid, *refs),
-        out_shape=(full, full, full),
+    return pl.pallas_call(
+        lambda *refs: advance_kernel(merid, *refs),
+        out_shape=(flat, flat, flat, full, full, full),
         in_specs=[VMEM] * 9,
-        out_specs=(VMEM,) * 3,
-        scratch_shapes=[pltpu.VMEM((3 * layers, short, cols + LANES), f32)],
-        name="layers",
-    )(thickness, velocity_u, velocity_v, deep_from_east, deep_from_west, from_north, from_south, folded, shared)
-    return eta, bu, bv, h, u, v
+        out_specs=(VMEM,) * 6,
+        scratch_shapes=[
+            pltpu.VMEM((4 + 2 * STEPS, short, cols + LANES), f32),
+            pltpu.VMEM((FIELDS, tall, cols + LANES), f32),
+            pltpu.VMEM((3 * layers, short, cols + LANES), f32),
+        ],
+        name="advance",
+    )(fields, thickness, velocity_u, velocity_v, wide_from_east, wide_from_west, from_north, from_south, folded)
 
 
 def solution(mesh):

time: 53 us -> 43.8 us (0.83)
  starting transfers between devices: 21.9 us -> 13.4 us
  Pallas kernels: 19.2 us -> 14.8 us
  waiting for transfers between devices: 8.94 us -> 13.2 us
  local copies, waits for them, and re-layouts: 1.98 us -> 1.41 us
    ppermute x1, waiting for transfers between devices: 0.87 us -> 10.6 us  [body(): strips_from_east = lax.ppermute(strips_west, 'zonal', down)]
    ppermute x1, waiting for transfers between devices: 5.49 us -> 0.01 us  [body(): strips_from_west = lax.ppermute(strips_east, 'zonal', up)]
    pallas_call x3 -> x1, Pallas kernels: 14.9 us -> 10.4 us  [body(): pl.pallas_call(lambda *refs: advance_kernel(merid, *refs), out_shape=(fla...]
    ppermute x2 -> x0, starting transfers between devices: 4.21 us -> none  [the longest x1 4.21 us: body(): deep_from_east = lax.ppermute(deep_west, 'zonal', down)]
    ppermute x1, starting transfers between devices: 0.01 us -> 2.06 us  [body(): wide_from_west = lax.ppermute(wide_east, 'zonal', up)]
    ppermute x1, starting transfers between devices: 5.11 us -> 3.1 us  [body(): wide_from_east = lax.ppermute(wide_west, 'zonal', down)]
    ppermute x1, starting transfers between devices: 3.25 us -> 1.4 us  [body(): strips_from_east = lax.ppermute(strips_west, 'zonal', down)]
    ppermute x1, starting transfers between devices: 6.61 us -> 4.92 us  [body(): folded = lax.ppermute(fold, ('zonal', 'merid'), mirror)]
  transfers between devices with their start and end apart: 8 -> 6, of which waited for: 4 -> 2; matrix products, arithmetic and copies ran while one was open for 0% -> 0% of each run, Pallas kernels for 15% -> 4%
where the time goes in v3:
time: 43.8 us; the launch traced here: 43.5 us
  Pallas kernels  14.8 us (34%)
  starting transfers between devices  13.4 us (31%)
  waiting for transfers between devices  13.2 us (30%)
  local copies, waits for them, and re-layouts  1.41 us (3%)
  between operations  0.69 us (2%)
    ppermute x1, waiting for transfers between devices, body(): strips_from_east = lax.ppermute(strips_west, 'zonal', down)  10.6 us
    pallas_call x1, Pallas kernels, body(): pl.pallas_call(lambda *refs: advance_kernel(merid, *refs), out_shape=(fla...  10.4 us
    ppermute x1, starting transfers between devices, body(): folded = lax.ppermute(fold, ('zonal', 'merid'), mirror)  4.92 us
    ppermute x1, starting transfers between devices, body(): wide_from_east = lax.ppermute(wide_west, 'zonal', down)  3.1 us
    ppermute x1, waiting for transfers between devices, body(): folded = lax.ppermute(fold, ('zonal', 'merid'), mirror)  2.6 us
    pallas_call x1, Pallas kernels, body(): pl.pallas_call(lambda *refs: prepare_kernel(rows * zonal, cols * merid, *...  2.57 us
    ppermute x1, starting transfers between devices, body(): wide_from_west = lax.ppermute(wide_east, 'zonal', up)  2.06 us
    pallas_call x1, Pallas kernels, body(): pl.pallas_call(lambda *refs: pack_kernel(merid, *refs), out_shape=(shape(...  1.84 us
  transfers between devices with their start and end apart: 6, of which 2 were waited for; matrix products, arithmetic and copies ran while one was open for 0% of the time, Pallas kernels for 4%

profile of v3, /device:TPU:1, one launch (start us, length us, event | category | flops | bytes accessed | tf_op | source)
XLA Modules:
  0.0 43.5 jit_solution(16003902456960861864)
XLA Ops:
  0.6 2.6 %prepare.1 = (f32[8,16,512]{2,1,0:T(8,128)}, f32[138,512]{1,0:T(8,128)}, f32[152,512]{1,0:T(8,128)}, f32[4,16,128]{2,1,0:T(8,128)}, f32[32,128]{1,0:T(8,128)}, /*index=5*/f32[32,128]{1,0:T(8,128)}) custom-call(s32[2,4]{1,0:T(2,128)} %bitcast.1, f32[4]{0:T(128)} %refs_1_.2, f32[16,512]{1,0:T(8,128)} %refs_2_.2, f32[16,512]{1,0:T(8,128)} %refs_3_.2, ...), custom_call_target="tpu_custom_call" | custom-call | tf_op jit(solution)/shard_map/prepare/pallas_call | solution.py:383
  3.2 2.1 %collective-permute-start.1 = (f32[152,512]{1,0:T(8,128)}, f32[152,512]{1,0:T(8,128)S(1)}, u32[]{:S(2)}, u32[]{:S(2)}) collective-permute-start(f32[152,512]{1,0:T(8,128)} %get-tuple-element.16), channel_id=1, source_target_pairs={{0,2},{2,4},{4,6},{6,8},{8,10},{10,12},{12,14},{14,0},{1,3},{3,5},... | collective-permute-start | bytes 933896 | tf_op jit(solution)/shard_map/ppermute | solution.py:403
  5.3 3.1 %collective-permute-start = (f32[138,512]{1,0:T(8,128)}, f32[138,512]{1,0:T(8,128)S(1)}, u32[]{:S(2)}, u32[]{:S(2)}) collective-permute-start(f32[138,512]{1,0:T(8,128)} %get-tuple-element.15), channel_id=1, source_target_pairs={{2,0},{4,2},{6,4},{8,6},{10,8},{12,10},{14,12},{0,14},{3,1},{5,3},... | collective-permute-start | bytes 847880 | tf_op jit(solution)/shard_map/ppermute | solution.py:402
  8.4 1.4 %collective-permute-start.2 = (f32[32,128]{1,0:T(8,128)}, f32[32,128]{1,0:T(8,128)S(1)}, u32[]{:S(2)}, u32[]{:S(2)}) collective-permute-start(f32[32,128]{1,0:T(8,128)} %get-tuple-element.18), channel_id=1, source_target_pairs={{2,0},{4,2},{6,4},{8,6},{10,8},{12,10},{14,12},{0,14},{3,1},{5,3},... | collective-permute-start | bytes 49160 | tf_op jit(solution)/shard_map/ppermute | solution.py:400
  9.8 0.1 collective-permute-start.3
  9.8 10.6 %collective-permute-done.2.refs_1_ = f32[32,128]{1,0:T(8,128)S(1)} collective-permute-done((f32[32,128]{1,0:T(8,128)}, f32[32,128]{1,0:T(8,128)S(1)}, u32[]{:S(2)}, u32[]{:S(2)}) %collective-permute-start.2) | collective-permute-done | bytes 16416 | tf_op jit(solution)/shard_map/ppermute | solution.py:400
  20.5 0.0 copy-start.4
  20.5 0.0 collective-permute-done.3.refs_2_
  20.5 0.6 %copy-done.4 = f32[32,128]{1,0:T(8,128)} copy-done((f32[32,128]{1,0:T(8,128)}, f32[32,128]{1,0:T(8,128)S(1)}, u32[]{:S(2)}) %copy-start.4) | copy-done | bytes 16408
  21.1 0.0 copy-done.5
  21.1 1.8 %pack.1 = (f32[64,128]{1,0:T(8,128)}, f32[64,128]{1,0:T(8,128)}, f32[64,128]{1,0:T(8,128)}) custom-call(f32[4,16,128]{2,1,0:T(8,128)} %get-tuple-element.17.refs_0_, f32[32,128]{1,0:T(8,128)} %copy-done.4, f32[32,128]{1,0:T(8,128)} %copy-done.5), custom_call_target="tpu_custom_call" | custom-call | tf_op jit(solution)/shard_map/pack/pallas_call | solution.py:405
  22.9 1.8 %collective-permute-start.4 = (f32[64,128]{1,0:T(8,128)}, f32[64,128]{1,0:T(8,128)S(1)}, u32[]{:S(2)}, u32[]{:S(2)}) collective-permute-start(f32[64,128]{1,0:T(8,128)} %get-tuple-element.20), channel_id=1, source_target_pairs={{0,1},{1,0},{2,3},{3,2},{4,5},{5,4},{6,7},{7,6},{8,9},{9,8},{10,11... | collective-permute-start | bytes 98312 | tf_op jit(solution)/shard_map/ppermute | solution.py:416
  24.7 4.9 %collective-permute-start.5 = (f32[64,128]{1,0:T(8,128)}, f32[64,128]{1,0:T(8,128)S(1)}, u32[]{:S(2)}, u32[]{:S(2)}) collective-permute-start(f32[64,128]{1,0:T(8,128)} %get-tuple-element.21), channel_id=1, source_target_pairs={{1,15},{3,13},{5,11},{7,9},{9,7},{11,5},{13,3},{15,1},{17,31},{19,... | collective-permute-start | bytes 98312 | tf_op jit(solution)/shard_map/ppermute | solution.py:414
  29.7 0.0 collective-permute-done.4.refs_6_.refs_7_
  29.7 0.0 copy-start.2
  29.7 2.6 %collective-permute-done.5.refs_8_ = f32[64,128]{1,0:T(8,128)S(1)} collective-permute-done((f32[64,128]{1,0:T(8,128)}, f32[64,128]{1,0:T(8,128)S(1)}, u32[]{:S(2)}, u32[]{:S(2)}) %collective-permute-start.5) | collective-permute-done | bytes 32800 | tf_op jit(solution)/shard_map/ppermute | solution.py:414
  32.3 0.0 collective-permute-done.refs_4_
  32.3 0.0 collective-permute-done.1.refs_5_
  32.3 0.0 copy-start
  32.3 0.0 copy-done.2
  32.3 0.6 %copy-done.3 = f32[64,128]{1,0:T(8,128)} copy-done((f32[64,128]{1,0:T(8,128)}, f32[64,128]{1,0:T(8,128)S(1)}, u32[]{:S(2)}) %copy-start.3) | copy-done | bytes 32792
  32.9 0.1 copy-done.1
  33.0 0.1 copy-done
  33.1 10.4 %advance.1 = (f32[16,512]{1,0:T(8,128)}, f32[16,512]{1,0:T(8,128)}, f32[16,512]{1,0:T(8,128)}, f32[14,16,512]{2,1,0:T(8,128)}, f32[14,16,512]{2,1,0:T(8,128)}, /*index=5*/f32[14,16,512]{2,1,0:T(8,128)}) custom-call(f32[8,16,512]{2,1,0:T(8,128)} %get-tuple-element.14.refs_0_, f32[14,16,512]{2,1,0:T(8,128)} %refs_1_.3, f32[14,16,512]{2,1,0:T(8,128)} %refs_2_.3, ...), custom_call_target="tpu_custom_call" | custom-call | tf_op jit(solution)/shard_map/advance/pallas_call | solution.py:424
  (3 shorter events, 0.0 us)
Async XLA Ops:
  3.2 29.1 %collective-permute-start.1 = (f32[152,512]{1,0:T(8,128)}, f32[152,512]{1,0:T(8,128)S(1)}, u32[]{:S(2)}, u32[]{:S(2)}) collective-permute-start(f32[152,512]{1,0:T(8,128)} %get-tuple-element.16), channel_id=1, source_target_pairs={{0,2},{2,4},{4,6},{6,8},{8,10},{10,12},{12,14},{14,0},{1,3},{3,5},... | collective-permute-start | bytes 933896 | tf_op jit(solution)/shard_map/ppermute | solution.py:403
  5.3 27.0 %collective-permute-start = (f32[138,512]{1,0:T(8,128)}, f32[138,512]{1,0:T(8,128)S(1)}, u32[]{:S(2)}, u32[]{:S(2)}) collective-permute-start(f32[138,512]{1,0:T(8,128)} %get-tuple-element.15), channel_id=1, source_target_pairs={{2,0},{4,2},{6,4},{8,6},{10,8},{12,10},{14,12},{0,14},{3,1},{5,3},... | collective-permute-start | bytes 847880 | tf_op jit(solution)/shard_map/ppermute | solution.py:402
  8.4 12.1 %collective-permute-start.2 = (f32[32,128]{1,0:T(8,128)}, f32[32,128]{1,0:T(8,128)S(1)}, u32[]{:S(2)}, u32[]{:S(2)}) collective-permute-start(f32[32,128]{1,0:T(8,128)} %get-tuple-element.18), channel_id=1, source_target_pairs={{2,0},{4,2},{6,4},{8,6},{10,8},{12,10},{14,12},{0,14},{3,1},{5,3},... | collective-permute-start | bytes 49160 | tf_op jit(solution)/shard_map/ppermute | solution.py:400
  9.8 10.7 %collective-permute-start.3 = (f32[32,128]{1,0:T(8,128)}, f32[32,128]{1,0:T(8,128)S(1)}, u32[]{:S(2)}, u32[]{:S(2)}) collective-permute-start(f32[32,128]{1,0:T(8,128)} %get-tuple-element.19), channel_id=1, source_target_pairs={{0,2},{2,4},{4,6},{6,8},{8,10},{10,12},{12,14},{14,0},{1,3},{3,5},... | collective-permute-start | bytes 49160 | tf_op jit(solution)/shard_map/ppermute | solution.py:401
  20.5 0.6 %copy-start.4 = (f32[32,128]{1,0:T(8,128)}, f32[32,128]{1,0:T(8,128)S(1)}, u32[]{:S(2)}) copy-start(f32[32,128]{1,0:T(8,128)S(1)} %collective-permute-done.2.refs_1_) | copy-start | bytes 49156
  20.5 0.6 %copy-start.5 = (f32[32,128]{1,0:T(8,128)}, f32[32,128]{1,0:T(8,128)S(1)}, u32[]{:S(2)}) copy-start(f32[32,128]{1,0:T(8,128)S(1)} %collective-permute-done.3.refs_2_) | copy-start | bytes 49156
  22.9 6.7 %collective-permute-start.4 = (f32[64,128]{1,0:T(8,128)}, f32[64,128]{1,0:T(8,128)S(1)}, u32[]{:S(2)}, u32[]{:S(2)}) collective-permute-start(f32[64,128]{1,0:T(8,128)} %get-tuple-element.20), channel_id=1, source_target_pairs={{0,1},{1,0},{2,3},{3,2},{4,5},{5,4},{6,7},{7,6},{8,9},{9,8},{10,11... | collective-permute-start | bytes 98312 | tf_op jit(solution)/shard_map/ppermute | solution.py:416
  24.7 7.6 %collective-permute-start.5 = (f32[64,128]{1,0:T(8,128)}, f32[64,128]{1,0:T(8,128)S(1)}, u32[]{:S(2)}, u32[]{:S(2)}) collective-permute-start(f32[64,128]{1,0:T(8,128)} %get-tuple-element.21), channel_id=1, source_target_pairs={{1,15},{3,13},{5,11},{7,9},{9,7},{11,5},{13,3},{15,1},{17,31},{19,... | collective-permute-start | bytes 98312 | tf_op jit(solution)/shard_map/ppermute | solution.py:414
  29.7 2.6 %copy-start.2 = (f32[64,128]{1,0:T(8,128)}, f32[64,128]{1,0:T(8,128)S(1)}, u32[]{:S(2)}) copy-start(f32[64,128]{1,0:T(8,128)S(1)} %collective-permute-done.4.refs_6_.refs_7_) | copy-start | bytes 98308
  32.3 0.6 %copy-start.3 = (f32[64,128]{1,0:T(8,128)}, f32[64,128]{1,0:T(8,128)S(1)}, u32[]{:S(2)}) copy-start(f32[64,128]{1,0:T(8,128)S(1)} %collective-permute-done.5.refs_8_) | copy-start | bytes 98308
  32.3 0.7 %copy-start.1 = (f32[138,512]{1,0:T(8,128)}, f32[138,512]{1,0:T(8,128)S(1)}, u32[]{:S(2)}) copy-start(f32[138,512]{1,0:T(8,128)S(1)} %collective-permute-done.refs_4_) | copy-start | bytes 847876
  32.3 0.8 %copy-start = (f32[152,512]{1,0:T(8,128)}, f32[152,512]{1,0:T(8,128)S(1)}, u32[]{:S(2)}) copy-start(f32[152,512]{1,0:T(8,128)S(1)} %collective-permute-done.1.refs_5_) | copy-start | bytes 933892

commit v4 on v3

--- a/solution.py
+++ b/solution.py
@@ -292,8 +292,8 @@
         down = pltpu.roll(deep_s, (LANES - 2 - 2 * k) % LANES, 1)
         edge = jnp.where(lanes[short] >= LANES - 2, down, 0.0)
         deep[k, :, cols:] = jnp.where(lanes[short] < 2, up, edge)
-    spot = lax.broadcasted_iota(jnp.int32, (short, cols), 0)
-    given = jnp.logical_or(spot == rows, spot == short - 2)
+    spot = lax.broadcasted_iota(jnp.int32, (EDGE, cols), 0)
+    given = jnp.logical_or(spot == 0, spot == EDGE - 2)
 
     for step in range(STEPS):
         last = step == STEPS - 1
@@ -313,7 +313,9 @@
             trial_v = v - PRESS_COEF * press_v
             flux_u = u * thick_u
             if not last:
-                flux_u = jnp.concatenate([jnp.where(given, u[:, :cols], flux_u[:, :cols]), flux_u[:, cols:]], axis=1)
+                outer = jnp.where(given, u[rows:, :cols], flux_u[rows:, :cols])
+                inside = jnp.concatenate([flux_u[:rows, :cols], outer], axis=0)
+                flux_u = jnp.concatenate([inside, flux_u[:, cols:]], axis=1)
             flux_v = v * thick_v
             new = h - FLUX_STEP * (flux_u - west(flux_u) + flux_v - south(flux_v))
             if last:

time: 43.8 us -> 43.8 us (level)
  no operation moved by 1% of the time
where the time goes in v4:
time: 43.8 us; the launch traced here: 43.5 us
  Pallas kernels  14.8 us (34%)
  starting transfers between devices  13.4 us (31%)
  waiting for transfers between devices  13.2 us (30%)
  local copies, waits for them, and re-layouts  1.41 us (3%)
  between operations  0.69 us (2%)
    ppermute x1, waiting for transfers between devices, body(): strips_from_east = lax.ppermute(strips_west, 'zonal', down)  10.6 us
    pallas_call x1, Pallas kernels, body(): pl.pallas_call(lambda *refs: advance_kernel(merid, *refs), out_shape=(fla...  10.4 us
    ppermute x1, starting transfers between devices, body(): folded = lax.ppermute(fold, ('zonal', 'merid'), mirror)  4.92 us
    ppermute x1, starting transfers between devices, body(): wide_from_east = lax.ppermute(wide_west, 'zonal', down)  3.1 us
    ppermute x1, waiting for transfers between devices, body(): folded = lax.ppermute(fold, ('zonal', 'merid'), mirror)  2.6 us
    pallas_call x1, Pallas kernels, body(): pl.pallas_call(lambda *refs: prepare_kernel(rows * zonal, cols * merid, *...  2.57 us
    ppermute x1, starting transfers between devices, body(): wide_from_west = lax.ppermute(wide_east, 'zonal', up)  2.06 us
    pallas_call x1, Pallas kernels, body(): pl.pallas_call(lambda *refs: pack_kernel(merid, *refs), out_shape=(shape(...  1.84 us
  transfers between devices with their start and end apart: 6, of which 2 were waited for; matrix products, arithmetic and copies ran while one was open for 0% of the time, Pallas kernels for 4%

profile of v4, /device:TPU:1, one launch (start us, length us, event | category | flops | bytes accessed | tf_op | source)
XLA Modules:
  0.0 43.5 jit_solution(930172998229569819)
XLA Ops:
  0.6 2.6 %prepare.1 = (f32[8,16,512]{2,1,0:T(8,128)}, f32[138,512]{1,0:T(8,128)}, f32[152,512]{1,0:T(8,128)}, f32[4,16,128]{2,1,0:T(8,128)}, f32[32,128]{1,0:T(8,128)}, /*index=5*/f32[32,128]{1,0:T(8,128)}) custom-call(s32[2,4]{1,0:T(2,128)} %bitcast.1, f32[4]{0:T(128)} %refs_1_.2, f32[16,512]{1,0:T(8,128)} %refs_2_.2, f32[16,512]{1,0:T(8,128)} %refs_3_.2, ...), custom_call_target="tpu_custom_call" | custom-call | tf_op jit(solution)/shard_map/prepare/pallas_call | solution.py:385
  3.2 2.1 %collective-permute-start.1 = (f32[152,512]{1,0:T(8,128)}, f32[152,512]{1,0:T(8,128)S(1)}, u32[]{:S(2)}, u32[]{:S(2)}) collective-permute-start(f32[152,512]{1,0:T(8,128)} %get-tuple-element.16), channel_id=1, source_target_pairs={{0,2},{2,4},{4,6},{6,8},{8,10},{10,12},{12,14},{14,0},{1,3},{3,5},... | collective-permute-start | bytes 933896 | tf_op jit(solution)/shard_map/ppermute | solution.py:405
  5.3 3.1 %collective-permute-start = (f32[138,512]{1,0:T(8,128)}, f32[138,512]{1,0:T(8,128)S(1)}, u32[]{:S(2)}, u32[]{:S(2)}) collective-permute-start(f32[138,512]{1,0:T(8,128)} %get-tuple-element.15), channel_id=1, source_target_pairs={{2,0},{4,2},{6,4},{8,6},{10,8},{12,10},{14,12},{0,14},{3,1},{5,3},... | collective-permute-start | bytes 847880 | tf_op jit(solution)/shard_map/ppermute | solution.py:404
  8.4 1.4 %collective-permute-start.2 = (f32[32,128]{1,0:T(8,128)}, f32[32,128]{1,0:T(8,128)S(1)}, u32[]{:S(2)}, u32[]{:S(2)}) collective-permute-start(f32[32,128]{1,0:T(8,128)} %get-tuple-element.18), channel_id=1, source_target_pairs={{2,0},{4,2},{6,4},{8,6},{10,8},{12,10},{14,12},{0,14},{3,1},{5,3},... | collective-permute-start | bytes 49160 | tf_op jit(solution)/shard_map/ppermute | solution.py:402
  9.8 0.1 collective-permute-start.3
  9.8 10.6 %collective-permute-done.2.refs_1_ = f32[32,128]{1,0:T(8,128)S(1)} collective-permute-done((f32[32,128]{1,0:T(8,128)}, f32[32,128]{1,0:T(8,128)S(1)}, u32[]{:S(2)}, u32[]{:S(2)}) %collective-permute-start.2) | collective-permute-done | bytes 16416 | tf_op jit(solution)/shard_map/ppermute | solution.py:402
  20.5 0.0 copy-start.4
  20.5 0.0 collective-permute-done.3.refs_2_
  20.5 0.6 %copy-done.4 = f32[32,128]{1,0:T(8,128)} copy-done((f32[32,128]{1,0:T(8,128)}, f32[32,128]{1,0:T(8,128)S(1)}, u32[]{:S(2)}) %copy-start.4) | copy-done | bytes 16408
  21.1 0.0 copy-done.5
  21.1 1.8 %pack.1 = (f32[64,128]{1,0:T(8,128)}, f32[64,128]{1,0:T(8,128)}, f32[64,128]{1,0:T(8,128)}) custom-call(f32[4,16,128]{2,1,0:T(8,128)} %get-tuple-element.17.refs_0_, f32[32,128]{1,0:T(8,128)} %copy-done.4, f32[32,128]{1,0:T(8,128)} %copy-done.5), custom_call_target="tpu_custom_call" | custom-call | tf_op jit(solution)/shard_map/pack/pallas_call | solution.py:407
  22.9 1.8 %collective-permute-start.4 = (f32[64,128]{1,0:T(8,128)}, f32[64,128]{1,0:T(8,128)S(1)}, u32[]{:S(2)}, u32[]{:S(2)}) collective-permute-start(f32[64,128]{1,0:T(8,128)} %get-tuple-element.20), channel_id=1, source_target_pairs={{0,1},{1,0},{2,3},{3,2},{4,5},{5,4},{6,7},{7,6},{8,9},{9,8},{10,11... | collective-permute-start | bytes 98312 | tf_op jit(solution)/shard_map/ppermute | solution.py:418
  24.7 4.9 %collective-permute-start.5 = (f32[64,128]{1,0:T(8,128)}, f32[64,128]{1,0:T(8,128)S(1)}, u32[]{:S(2)}, u32[]{:S(2)}) collective-permute-start(f32[64,128]{1,0:T(8,128)} %get-tuple-element.21), channel_id=1, source_target_pairs={{1,15},{3,13},{5,11},{7,9},{9,7},{11,5},{13,3},{15,1},{17,31},{19,... | collective-permute-start | bytes 98312 | tf_op jit(solution)/shard_map/ppermute | solution.py:416
  29.7 0.0 collective-permute-done.4.refs_6_.refs_7_
  29.7 0.0 copy-start.2
  29.7 2.6 %collective-permute-done.5.refs_8_ = f32[64,128]{1,0:T(8,128)S(1)} collective-permute-done((f32[64,128]{1,0:T(8,128)}, f32[64,128]{1,0:T(8,128)S(1)}, u32[]{:S(2)}, u32[]{:S(2)}) %collective-permute-start.5) | collective-permute-done | bytes 32800 | tf_op jit(solution)/shard_map/ppermute | solution.py:416
  32.3 0.0 collective-permute-done.refs_4_
  32.3 0.0 collective-permute-done.1.refs_5_
  32.3 0.0 copy-start
  32.3 0.0 copy-done.2
  32.3 0.6 %copy-done.3 = f32[64,128]{1,0:T(8,128)} copy-done((f32[64,128]{1,0:T(8,128)}, f32[64,128]{1,0:T(8,128)S(1)}, u32[]{:S(2)}) %copy-start.3) | copy-done | bytes 32792
  32.9 0.1 copy-done.1
  33.0 0.1 copy-done
  33.1 10.4 %advance.1 = (f32[16,512]{1,0:T(8,128)}, f32[16,512]{1,0:T(8,128)}, f32[16,512]{1,0:T(8,128)}, f32[14,16,512]{2,1,0:T(8,128)}, f32[14,16,512]{2,1,0:T(8,128)}, /*index=5*/f32[14,16,512]{2,1,0:T(8,128)}) custom-call(f32[8,16,512]{2,1,0:T(8,128)} %get-tuple-element.14.refs_0_, f32[14,16,512]{2,1,0:T(8,128)} %refs_1_.3, f32[14,16,512]{2,1,0:T(8,128)} %refs_2_.3, ...), custom_call_target="tpu_custom_call" | custom-call | tf_op jit(solution)/shard_map/advance/pallas_call | solution.py:426
  (3 shorter events, 0.0 us)
Async XLA Ops:
  3.2 29.1 %collective-permute-start.1 = (f32[152,512]{1,0:T(8,128)}, f32[152,512]{1,0:T(8,128)S(1)}, u32[]{:S(2)}, u32[]{:S(2)}) collective-permute-start(f32[152,512]{1,0:T(8,128)} %get-tuple-element.16), channel_id=1, source_target_pairs={{0,2},{2,4},{4,6},{6,8},{8,10},{10,12},{12,14},{14,0},{1,3},{3,5},... | collective-permute-start | bytes 933896 | tf_op jit(solution)/shard_map/ppermute | solution.py:405
  5.3 27.0 %collective-permute-start = (f32[138,512]{1,0:T(8,128)}, f32[138,512]{1,0:T(8,128)S(1)}, u32[]{:S(2)}, u32[]{:S(2)}) collective-permute-start(f32[138,512]{1,0:T(8,128)} %get-tuple-element.15), channel_id=1, source_target_pairs={{2,0},{4,2},{6,4},{8,6},{10,8},{12,10},{14,12},{0,14},{3,1},{5,3},... | collective-permute-start | bytes 847880 | tf_op jit(solution)/shard_map/ppermute | solution.py:404
  8.4 12.1 %collective-permute-start.2 = (f32[32,128]{1,0:T(8,128)}, f32[32,128]{1,0:T(8,128)S(1)}, u32[]{:S(2)}, u32[]{:S(2)}) collective-permute-start(f32[32,128]{1,0:T(8,128)} %get-tuple-element.18), channel_id=1, source_target_pairs={{2,0},{4,2},{6,4},{8,6},{10,8},{12,10},{14,12},{0,14},{3,1},{5,3},... | collective-permute-start | bytes 49160 | tf_op jit(solution)/shard_map/ppermute | solution.py:402
  9.8 10.7 %collective-permute-start.3 = (f32[32,128]{1,0:T(8,128)}, f32[32,128]{1,0:T(8,128)S(1)}, u32[]{:S(2)}, u32[]{:S(2)}) collective-permute-start(f32[32,128]{1,0:T(8,128)} %get-tuple-element.19), channel_id=1, source_target_pairs={{0,2},{2,4},{4,6},{6,8},{8,10},{10,12},{12,14},{14,0},{1,3},{3,5},... | collective-permute-start | bytes 49160 | tf_op jit(solution)/shard_map/ppermute | solution.py:403
  20.5 0.6 %copy-start.4 = (f32[32,128]{1,0:T(8,128)}, f32[32,128]{1,0:T(8,128)S(1)}, u32[]{:S(2)}) copy-start(f32[32,128]{1,0:T(8,128)S(1)} %collective-permute-done.2.refs_1_) | copy-start | bytes 49156
  20.5 0.6 %copy-start.5 = (f32[32,128]{1,0:T(8,128)}, f32[32,128]{1,0:T(8,128)S(1)}, u32[]{:S(2)}) copy-start(f32[32,128]{1,0:T(8,128)S(1)} %collective-permute-done.3.refs_2_) | copy-start | bytes 49156
  22.9 6.7 %collective-permute-start.4 = (f32[64,128]{1,0:T(8,128)}, f32[64,128]{1,0:T(8,128)S(1)}, u32[]{:S(2)}, u32[]{:S(2)}) collective-permute-start(f32[64,128]{1,0:T(8,128)} %get-tuple-element.20), channel_id=1, source_target_pairs={{0,1},{1,0},{2,3},{3,2},{4,5},{5,4},{6,7},{7,6},{8,9},{9,8},{10,11... | collective-permute-start | bytes 98312 | tf_op jit(solution)/shard_map/ppermute | solution.py:418
  24.7 7.6 %collective-permute-start.5 = (f32[64,128]{1,0:T(8,128)}, f32[64,128]{1,0:T(8,128)S(1)}, u32[]{:S(2)}, u32[]{:S(2)}) collective-permute-start(f32[64,128]{1,0:T(8,128)} %get-tuple-element.21), channel_id=1, source_target_pairs={{1,15},{3,13},{5,11},{7,9},{9,7},{11,5},{13,3},{15,1},{17,31},{19,... | collective-permute-start | bytes 98312 | tf_op jit(solution)/shard_map/ppermute | solution.py:416
  29.7 2.6 %copy-start.2 = (f32[64,128]{1,0:T(8,128)}, f32[64,128]{1,0:T(8,128)S(1)}, u32[]{:S(2)}) copy-start(f32[64,128]{1,0:T(8,128)S(1)} %collective-permute-done.4.refs_6_.refs_7_) | copy-start | bytes 98308
  32.3 0.6 %copy-start.3 = (f32[64,128]{1,0:T(8,128)}, f32[64,128]{1,0:T(8,128)S(1)}, u32[]{:S(2)}) copy-start(f32[64,128]{1,0:T(8,128)S(1)} %collective-permute-done.5.refs_8_) | copy-start | bytes 98308
  32.3 0.7 %copy-start.1 = (f32[138,512]{1,0:T(8,128)}, f32[138,512]{1,0:T(8,128)S(1)}, u32[]{:S(2)}) copy-start(f32[138,512]{1,0:T(8,128)S(1)} %collective-permute-done.refs_4_) | copy-start | bytes 847876
  32.3 0.8 %copy-start = (f32[152,512]{1,0:T(8,128)}, f32[152,512]{1,0:T(8,128)S(1)}, u32[]{:S(2)}) copy-start(f32[152,512]{1,0:T(8,128)S(1)} %collective-permute-done.1.refs_5_) | copy-start | bytes 933892
